TPU v7x, 32 devices: a whole 2x2x4 slice. The times are simulated.
32 devices in a mesh: gx: 2 (over x), gy: 4 (over y, core), gz: 4 (over z).
Axes of the slice: x: 2, y: 2, z: 4, core: 2. Of those that a mesh axis runs over, the one named last changes fastest.
Arguments:
- atom_feat: bfloat16 [32768, 128], P(('gx', 'gy', 'gz')), may hold values from -6 to 6
- atom_env: bfloat16 [32768, 9, 128], P(('gx', 'gy', 'gz')), may hold values from -6 to 6
- export_index: int32 [8192], P(('gx', 'gy', 'gz')), may hold values from 0 to 1023
- pair_vec: float32 [3, 65536], P(None, ('gx', 'gy', 'gz')), may hold values from -8 to 8
- pair_center: int32 [65536], P(('gx', 'gy', 'gz')), may hold values from 0 to 1023
- pair_owner: int32 [65536, 1], P(('gx', 'gy', 'gz')), may hold values from 0 to 15; in each aligned block of 2048 rows (0 to 2047, 2048 to 4095, ...) at most 192 rows name the same one
- pair_neigh: int32 [65536], P(('gx', 'gy', 'gz')), may hold values from 0 to 7935
- pair_count: int32 [32], P(('gx', 'gy', 'gz')), may hold values from 512 to 2048
- center_proj: bfloat16 [128, 512], replicated, may hold values from -0.375 to 0.375
- neighbour_proj: bfloat16 [128, 512], replicated, may hold values from -0.375 to 0.375
- radial_proj: bfloat16 [8, 512], replicated, may hold values from -4 to 4
- hidden_proj: bfloat16 [512, 512], replicated, may hold values from -0.25 to 0.25
- split_proj: bfloat16 [512, 384], replicated, may hold values from -0.5 to 0.5
- scalar_proj: bfloat16 [384, 512], replicated, may hold values from -0.3125 to 0.3125
- path_gain: float32 [3, 128], replicated, may hold values from 0.1 to 1.9
- energy_proj: float32 [512], replicated, may hold values from -0.5 to 0.5
Outputs:
- pair_latent: bfloat16 [65536, 512], P(('gx', 'gy', 'gz'))
- pair_vector: bfloat16 [3, 65536, 128], P(None, ('gx', 'gy', 'gz'))
- atom_energy: float32 [32768], P(('gx', 'gy', 'gz'))
Inputs may be any that keep to these rules, and one draw needn't show every extreme that they name: `pair_owner`: among the pair slots of one device at most 192 name the same owner, a bound that some block reaches of them.
All inputs are finite; a program needn't handle non-finite values.
Results may differ from a plain program's by a relative error of at most 0.0062.
Values may be sent and summed in bfloat16 or wider, within the bound.
No kernel may reach another device: no remote copies, remote signals or barrier semaphores. Data moves between devices by JAX's collectives and lax.ppermute only.
A program may use at most 128 MiB of HBM per device.

v0:
```python
import jax
import jax.numpy as jnp
from jax import lax
from jax.sharding import PartitionSpec as P

cutoff = 6.0
root_two = 2.0**0.5
root_three = 3.0**0.5
root_five = 5.0**0.5
root_fifteen = 15.0**0.5


def with_halo(x, sides, width):
    for axis, dim in sides:
        size, length = (lax.axis_size(axis), x.shape[dim])
        up = [(i, (i + 1) % size) for i in range(size)]
        down = [(j, i) for i, j in up]
        last = lax.slice_in_dim(x, length - width, length, axis=dim)
        leading = lax.slice_in_dim(x, 0, width, axis=dim)
        before = lax.ppermute(last, axis, up)
        after = lax.ppermute(leading, axis, down)
        x = jnp.concatenate([before, x, after], axis=dim)
    return x


def pair_block(
    h_center,
    env_center,
    h_neighbour,
    geometry,
    live,
    center_proj,
    neighbour_proj,
    radial_proj,
    hidden_proj,
    split_proj,
    scalar_proj,
    path_gain,
    energy_proj,
):
    channels = h_center.shape[1]
    basis = radial_proj.shape[0]
    length = jnp.sqrt(jnp.sum(geometry * geometry, axis=0))
    unit = geometry / jnp.maximum(length, 1.0)[None, :]
    spacing = cutoff / (basis - 1)
    centres = jnp.arange(basis).astype(geometry.dtype) * spacing
    radial = jnp.exp(-jnp.square((length[:, None] - centres[None, :]) / spacing))
    before = jnp.dot(h_center, center_proj, preferred_element_type=jnp.float32)
    before = before + jnp.dot(h_neighbour, neighbour_proj, preferred_element_type=jnp.float32)
    before = before + jnp.dot(
        radial, radial_proj.astype(jnp.float32), precision=lax.Precision.HIGHEST
    )
    hidden = jax.nn.silu(before).astype(jnp.bfloat16)
    latent = jax.nn.silu(jnp.dot(hidden, hidden_proj, preferred_element_type=jnp.float32)).astype(
        jnp.bfloat16
    )
    mixed = jnp.dot(latent, split_proj, preferred_element_type=jnp.float32)
    scalar_part = mixed[:, :channels]
    vector_part = mixed[:, channels : 2 * channels]
    tensor_part = mixed[:, 2 * channels :]
    ux, uy, uz = (unit[0][:, None], unit[1][:, None], unit[2][:, None])
    first = [root_three * ux, root_three * uy, root_three * uz]
    second = [
        root_fifteen * ux * uy,
        root_fifteen * uy * uz,
        0.5 * root_five * (2.0 * uz * uz - ux * ux - uy * uy),
        root_fifteen * ux * uz,
        0.5 * root_fifteen * (ux * ux - uy * uy),
    ]
    env_scalar = env_center[:, 0, :].astype(jnp.float32)
    env_vector = [env_center[:, 1 + m, :].astype(jnp.float32) for m in range(3)]
    env_tensor = [env_center[:, 4 + m, :].astype(jnp.float32) for m in range(5)]
    edge_vector = [vector_part * first[m] for m in range(3)]
    vector_dot = (
        edge_vector[0] * env_vector[0]
        + edge_vector[1] * env_vector[1]
        + edge_vector[2] * env_vector[2]
    )
    tensor_dot = tensor_part * second[0] * env_tensor[0]
    for m in range(1, 5):
        tensor_dot = tensor_dot + tensor_part * second[m] * env_tensor[m]
    invariants = jnp.concatenate(
        [scalar_part * env_scalar, vector_dot / root_three, tensor_dot / root_five], axis=1
    ).astype(jnp.bfloat16)
    update = jax.nn.silu(jnp.dot(invariants, scalar_proj, preferred_element_type=jnp.float32))
    latent_out = jnp.where(live[:, None], latent.astype(jnp.float32) + update, 0.0).astype(
        jnp.bfloat16
    )
    cross = [
        edge_vector[1] * env_vector[2] - edge_vector[2] * env_vector[1],
        edge_vector[2] * env_vector[0] - edge_vector[0] * env_vector[2],
        edge_vector[0] * env_vector[1] - edge_vector[1] * env_vector[0],
    ]
    outputs = []
    for m in range(3):
        value = (
            path_gain[0][None, :] * scalar_part * env_vector[m]
            + path_gain[1][None, :] * edge_vector[m] * env_scalar
            + path_gain[2][None, :] * cross[m] / root_two
        )
        outputs.append(jnp.where(live[:, None], value, 0.0).astype(jnp.bfloat16))
    vector_out = jnp.stack(outputs)
    energy = jnp.sum(latent_out.astype(jnp.float32) * energy_proj[None, :], axis=1)
    energy = jnp.where(live, energy, 0.0)
    return (latent_out, vector_out, energy)


def local(
    atom_feat,
    atom_env,
    export_index,
    pair_vec,
    pair_center,
    pair_owner,
    pair_neigh,
    pair_count,
    center_proj,
    neighbour_proj,
    radial_proj,
    hidden_proj,
    split_proj,
    scalar_proj,
    path_gain,
    energy_proj,
):
    atoms_here = atom_feat.shape[0]
    pair_slots = pair_center.shape[0]
    channels = atom_feat.shape[1]
    owners = lax.axis_size("gy") * lax.axis_size("gz")
    capacity = 3 * pair_slots // (2 * owners)
    exported = atom_feat[export_index]
    shell = with_halo(exported[None, None, None], (("gx", 0), ("gy", 1), ("gz", 2)), 1)
    table = jnp.concatenate([atom_feat, shell.reshape(-1, channels)], axis=0)
    owner = pair_owner[:, 0]
    positions = jnp.arange(pair_slots, dtype=jnp.int32)
    member_of = jnp.arange(owners, dtype=jnp.int32)[:, None] == owner[None, :]
    strictly_before = (positions[:, None] < positions[None, :]).astype(jnp.bfloat16)
    earlier = jnp.dot(
        member_of.astype(jnp.bfloat16), strictly_before, preferred_element_type=jnp.float32
    )
    rank = jnp.sum(jnp.where(member_of, earlier, 0.0), axis=0).astype(jnp.int32)
    slot = owner * capacity + rank
    live = positions < pair_count[0]
    coded = (
        jnp.full((owners * capacity,), -1, jnp.int32).at[slot].set(jnp.where(live, pair_center, -1))
    )
    neigh_codes = jnp.zeros((owners * capacity,), jnp.int32).at[slot].set(pair_neigh)
    placed = jnp.zeros((3, owners * capacity), jnp.float32).at[:, slot].set(pair_vec)
    coded_in, neigh_in, placed_in = (
        lax.all_to_all(
            coded.reshape(1, owners, capacity),
            ("gy", "gz"),
            split_axis=1,
            concat_axis=1,
            tiled=True,
        ),
        lax.all_to_all(
            neigh_codes.reshape(1, owners, capacity),
            ("gy", "gz"),
            split_axis=1,
            concat_axis=1,
            tiled=True,
        ),
        lax.all_to_all(
            placed.reshape(3, owners, capacity),
            ("gy", "gz"),
            split_axis=1,
            concat_axis=1,
            tiled=True,
        ),
    )
    codes = coded_in.reshape(-1)
    valid = codes >= 0
    center_rows = jnp.maximum(codes, 0)
    geometry = placed_in.reshape(3, owners * capacity)
    latent_far, vector_far, energy_far = pair_block(
        atom_feat[center_rows],
        atom_env[center_rows],
        table[neigh_in.reshape(-1)],
        geometry,
        valid,
        center_proj,
        neighbour_proj,
        radial_proj,
        hidden_proj,
        split_proj,
        scalar_proj,
        path_gain,
        energy_proj,
    )
    atom_energy = jax.ops.segment_sum(energy_far, center_rows, num_segments=atoms_here)
    back_latent, back_vector = (
        lax.all_to_all(
            latent_far.reshape(1, owners, capacity, -1),
            ("gy", "gz"),
            split_axis=1,
            concat_axis=1,
            tiled=True,
        ),
        lax.all_to_all(
            vector_far.reshape(3, owners, capacity, channels),
            ("gy", "gz"),
            split_axis=1,
            concat_axis=1,
            tiled=True,
        ),
    )
    latent_out = back_latent.reshape(owners * capacity, -1)[slot]
    vector_out = back_vector.reshape(3, owners * capacity, channels)[:, slot]
    return (latent_out, vector_out, atom_energy)


def solution(mesh):
    placed = (
        P(("gx", "gy", "gz"), None),
        P(("gx", "gy", "gz"), None, None),
        P(("gx", "gy", "gz")),
        P(None, ("gx", "gy", "gz")),
        P(("gx", "gy", "gz")),
        P(("gx", "gy", "gz"), None),
        P(("gx", "gy", "gz")),
        P(("gx", "gy", "gz")),
        P(),
        P(),
        P(),
        P(),
        P(),
        P(),
        P(),
        P(),
    )
    return jax.shard_map(
        local,
        mesh=mesh,
        in_specs=placed,
        out_specs=(
            P(("gx", "gy", "gz"), None),
            P(None, ("gx", "gy", "gz"), None),
            P(("gx", "gy", "gz")),
        ),
        check_vma=False,
    )
```

profile of v0, /device:TPU:0, one launch (start us, length us, event | category | flops | bytes accessed | tf_op | source)
XLA Modules:
  0.0 342.4 jit_solution(4964449564306291259)
XLA Ops:
  0.6 0.8 compare_select_fusion.2
  1.5 1.7 gather_fusion.1
  3.2 3.0 collective-permute-start.1
  6.2 0.1 collective-permute-start
  6.3 1.7 fusion.42
  8.8 8.1 %scatter_custom_fusion = s32[3072]{0:T(1024)S(1)} fusion(s32[2048]{0:T(1024)S(1)} %bitcast.138, s32[2048]{0:T(1024)S(1)} %fusion.57, s32[]{:T(128)} %constant.18.clone.1), kind=kCustom, calls=%fused_computation.131 | custom fusion | bytes 12292 | tf_op jit(solution)/shard_map/scatter | solution.py:145
  16.8 0.7 reshape.245
  17.5 6.4 %all-to-all-start = ((s32[1,16,192]{2,0,1:T(1,128)}), s32[1,16,192]{2,0,1:T(1,128)S(1)}, u32[]{:S(2)}, u32[]{:S(2)}) async-start(s32[1,16,192]{2,0,1:T(1,128)} %reshape.245), calls=%async_computation | async-start | bytes 32768 | tf_op jit(solution)/shard_map/all_to_all | solution.py:150
  23.9 0.6 slice_bitcast_fusion.11
  24.5 0.5 convert_multiply_fusion.21
  25.0 8.2 %scatter_custom_fusion.1 = s32[3072]{0:T(1024)S(1)} fusion(s32[2048]{0:T(1024)S(1)} %bitcast.139, s32[2048]{0:T(1024)} %param.22, s32[]{:T(128)} %constant.21.clone.1), kind=kCustom, calls=%fused_computation.129 | custom fusion | bytes 12800 | tf_op jit(solution)/shard_map/scatter | solution.py:147
  33.3 0.7 reshape.247
  33.9 1.3 copy.41
  35.3 7.2 %scatter_custom_fusion.2 = f32[3,3072]{0,1:T(8,128)} fusion(s32[2048]{0:T(1024)S(1)} %bitcast.140, f32[2048,3]{1,0:T(8,128)} %copy.41, f32[]{:T(128)} %constant.20.clone.1), kind=kCustom, calls=%fused_computation.93 | custom fusion | bytes 37376 | tf_op jit(solution)/shard_map/scatter | solution.py:148
  42.4 2.7 copy.42
  45.1 6.1 %all-to-all-start.1 = ((s32[1,16,192]{2,0,1:T(1,128)}), s32[1,16,192]{2,0,1:T(1,128)}, u32[]{:S(2)}, u32[]{:S(2)}) async-start(s32[1,16,192]{2,0,1:T(1,128)} %reshape.247), calls=%async_computation.1 | async-start | bytes 32768 | tf_op jit(solution)/shard_map/all_to_all | solution.py:157
  51.2 0.1 maximum_reduce_fusion
  51.2 0.1 reshape.265
  51.3 0.6 copy-done.9
  51.9 0.6 broadcast_clamp_fusion.1
  52.5 10.6 %gather_fusion = bf16[3072,128]{1,0:T(8,128)(2,1)S(1)} fusion(bf16[1024,128]{1,0:T(8,128)(2,1)S(1)} %copy-done.2, s32[3072]{0:T(1024)} %broadcast_clamp_fusion.1), kind=kCustom, calls=%fused_computation | custom fusion | bytes 1585152 | tf_op jit(solution)/shard_map/gather | solution.py:177
  63.1 6.0 %all-to-all-start.2 = ((f32[3,16,192]{2,0,1:T(4,128)}), f32[3,16,192]{2,0,1:T(4,128)}, u32[]{:S(2)}, u32[]{:S(2)}) async-start(f32[3,16,192]{2,0,1:T(4,128)} %copy.42), calls=%async_computation.2 | async-start | bytes 131072 | tf_op jit(solution)/shard_map/all_to_all | solution.py:164
  69.2 1.4 reduce.3
  70.5 1.4 reshape.248
  71.9 0.7 compare_select_fusion
  72.6 0.6 broadcast_clamp_fusion
  73.2 45.3 %gather_fusion.3 = bf16[3072,9,128]{2,0,1:T(8,128)(2,1)} fusion(bf16[1024,9,128]{2,0,1:T(8,128)(2,1)S(1)} %copy-done, s32[3072]{0:T(1024)} %broadcast_clamp_fusion.1), kind=kCustom, calls=%fused_computation.3 | custom fusion | bytes 14168064 | tf_op jit(solution)/shard_map/gather | solution.py:178
  118.6 4.6 %fusion.66 = f32[3072,512]{1,0:T(8,128)} fusion(bf16[3072,128]{1,0:T(8,128)(2,1)S(1)} %gather_fusion, bf16[128,512]{1,0:T(8,128)(2,1)} %param.24), kind=kOutput, calls=%fused_computation.145 | convolution fusion | flops 402653184 | bytes 7208960 | tf_op jit(solution)/shard_map/dot_general | solution.py:48
  123.1 0.1 compare_reduce_fusion
  123.2 0.1 ge.11
  123.3 0.9 pad_maximum_fusion.4
  124.1 1.6 collective-permute-start.3
  125.8 0.9 multiply_reduce_fusion.1
  126.7 0.1 sqrt.15
  126.7 0.9 copy.43
  127.6 0.1 reshape.250
  127.7 3.2 collective-permute-done.3
  130.9 1.0 collective-permute-done.2
  131.9 0.9 pad_maximum_fusion.3
  132.8 3.5 %collective-permute-start.5 = (bf16[3,3,1,256,128]{4,3,2,1,0:T(8,128)(2,1)S(1)}, bf16[3,3,1,256,128]{4,3,2,1,0:T(8,128)(2,1)S(1)}, u32[]{:S(2)}, u32[]{:S(2)}) collective-permute-start(bf16[3,3,1,256,128]{4,3,2,1,0:T(8,128)(2,1)S(1)} %pad_maximum_fusion.3), channel_id=1, source_target_pairs={{1,0},{2,1},{3,2},{0,3},{5,4},{6,5},{7,6},{4,7},{9,8},{10,9},{11,1... | collective-permute-start | bytes 1769480 | tf_op jit(solution)/shard_map/ppermute | solution.py:21
  136.4 13.6 %collective-permute-done.5 = bf16[3,3,1,256,128]{4,3,2,1,0:T(8,128)(2,1)S(1)} collective-permute-done((bf16[3,3,1,256,128]{4,3,2,1,0:T(8,128)(2,1)S(1)}, bf16[3,3,1,256,128]{4,3,2,1,0:T(8,128)(2,1)S(1)}, u32[]{:S(2)}, u32[]{:S(2)}) %collective-permute-start.5) | collective-permute-done | bytes 589856 | tf_op jit(solution)/shard_map/ppermute | solution.py:21
  150.1 11.9 %collective-permute-done.4 = bf16[3,3,1,256,128]{4,3,2,1,0:T(8,128)(2,1)S(1)} collective-permute-done((bf16[3,3,1,256,128]{4,3,2,1,0:T(8,128)(2,1)S(1)}, bf16[3,3,1,256,128]{4,3,2,1,0:T(8,128)(2,1)S(1)}, u32[]{:S(2)}, u32[]{:S(2)}) %collective-permute-start.4) | collective-permute-done | bytes 589856 | tf_op jit(solution)/shard_map/ppermute | solution.py:20
  161.9 1.0 pad_maximum_fusion.2
  163.0 0.1 pad_maximum_fusion.1
  163.1 0.6 copy-done.10
  163.7 9.1 %gather_fusion.2 = bf16[3072,128]{1,0:T(8,128)(2,1)S(1)} fusion(bf16[7936,128]{1,0:T(8,128)(2,1)S(1)} %pad_maximum_fusion.1, s32[3072]{0:T(1024)S(1)} %copy-done.10), kind=kCustom, calls=%fused_computation.2 | custom fusion | bytes 1585152 | tf_op jit(solution)/shard_map/gather | solution.py:179
  172.8 1.0 fusion.67
  173.8 6.5 %multiply_convert_fusion.1 = bf16[3072,512]{1,0:T(8,128)(2,1)S(1)} fusion(f32[3072,512]{1,0:T(8,128)} %fusion.66, f32[3072,512]{1,0:T(8,128)S(1)} %fusion.67, bf16[8,512]{1,0:T(8,128)(2,1)S(1)} %copy-done.22, f32[8]{0:T(128)S(1)} %copy-done.24, f32[3072]{0:T(1024)S(1)} %sqrt.15), kind=kOutput, calls=%fused_computation.15 | convolution fusion | flops 162103296 | bytes 15749152 | tf_op jit(solution)/shard_map/dot_general | solution.py:50
  180.4 2.7 multiply_convert_fusion
  183.1 1.8 fusion.68
  185.0 4.8 %fusion.27 = (bf16[3072,128]{1,0:T(8,128)(2,1)S(1)}, bf16[3072,128]{1,0:T(8,128)(2,1)S(1)}, bf16[3072,128]{1,0:T(8,128)(2,1)}) fusion(f32[3072,384]{1,0:T(8,128)S(1)} %fusion.68, f32[128]{0:T(128)S(1)} %copy-done.17, f32[128]{0:T(128)S(1)} %copy-done.18, f32[128]{0:T(128)S(1)} %copy-done.16, f32[3072]{0:T(1024)S(1)} %get-tuple-element.29, ...), kind=kLoop, calls=%fused_computation.61 | loop fusion | flops 11403264 | bytes 8692224 | tf_op jit(solution)/shard_map/convert_element_type | solution.py:101
  189.8 3.0 fusion.15
  192.8 1.6 pad_maximum_fusion
  194.4 4.9 %all-to-all-start.4 = ((bf16[3,16,192,128]{3,2,0,1:T(8,128)(2,1)}), bf16[3,16,192,128]{3,2,0,1:T(8,128)(2,1)S(1)}, u32[]{:S(2)}, u32[]{:S(2)}) async-start(bf16[3,16,192,128]{3,2,0,1:T(8,128)(2,1)} %pad_maximum_fusion), calls=%async_computation.4 | async-start | bytes 4718592 | tf_op jit(solution)/shard_map/all_to_all | solution.py:200
  199.3 5.7 %fusion.36 = bf16[3072,128]{1,0:T(8,128)(2,1)S(1)} fusion(f32[3072,384]{1,0:T(8,128)} %copy-done.3, bf16[3072,9,128]{2,0,1:T(8,128)(2,1)} %gather_fusion.3, f32[3072]{0:T(1024)S(1)} %get-tuple-element.27, f32[3072]{0:T(1024)S(1)} %get-tuple-element.30, f32[3072]{0:T(1024)S(1)} %get-tuple-element.26, f32[3072]{0:T(1024)S(1)} %get-tuple-element.25, ...), kind=kLoop, calls=%fused_computation.71 | loop fusion | flops 8257536 | bytes 6352896 | tf_op jit(solution)/shard_map/convert.11
  205.1 5.3 %multiply_reduce_fusion = (f32[3072]{0:T(1024)S(1)}, bf16[3072,512]{1,0:T(8,128)(2,1)}) fusion(f32[512]{0:T(512)S(1)} %copy-done.23, bf16[384,512]{1,0:T(8,128)(2,1)S(1)} %copy-done.21, bf16[3072,128]{1,0:T(8,128)(2,1)S(1)} %fusion.36, bf16[3072,128]{1,0:T(8,128)(2,1)S(1)} %get-tuple-element.18, bf16[3072,128]{1,0:T(8,128)(2,1)S(1)} %copy-done.6, ...), kind=kOutput, calls=%fused_computation.12 | convolution fusion | flops 1232335872 | bytes 9061376 | tf_op jit(solution)/shard_map/dot_general | solution.py:85
  210.4 43.9 %all-to-all-done.4 = bf16[3,16,192,128]{3,2,0,1:T(8,128)(2,1)S(1)} async-done(((bf16[3,16,192,128]{3,2,0,1:T(8,128)(2,1)}), bf16[3,16,192,128]{3,2,0,1:T(8,128)(2,1)S(1)}, u32[]{:S(2)}, u32[]{:S(2)}) %all-to-all-start.4) | async-done | bytes 2359328 | tf_op jit(solution)/shard_map/all_to_all | solution.py:200
  254.2 4.6 %all-to-all-start.3 = ((bf16[1,16,192,512]{3,2,0,1:T(8,128)(2,1)}), bf16[1,16,192,512]{3,2,0,1:T(8,128)(2,1)}, u32[]{:S(2)}, u32[]{:S(2)}) async-start(bf16[1,16,192,512]{3,2,0,1:T(8,128)(2,1)} %bitcast.124), calls=%async_computation.3 | async-start | bytes 6291456 | tf_op jit(solution)/shard_map/all_to_all | solution.py:193
  258.9 22.5 %scatter_custom_fusion.3 = f32[1024]{0:T(1024)} fusion(s32[3072]{0:T(1024)} %copy-done.9, f32[3072]{0:T(1024)S(1)} %broadcast_select_fusion, f32[]{:T(128)} %constant.20.clone.1), kind=kCustom, calls=%fused_computation.136 | custom fusion | flops 3072 | bytes 4608 | tf_op jit(solution)/shard_map/scatter-add | solution.py:191
  281.4 3.7 %copy.48 = bf16[3,16,192,128]{3,0,2,1:T(4,128)(2,1)} copy(bf16[3,16,192,128]{3,2,0,1:T(8,128)(2,1)S(1)} %all-to-all-done.4) | data formatting | bytes 4718592 | tf_op jit(solution)/shard_map/all_to_all | solution.py:200
  285.1 8.7 %gather_fusion.5 = bf16[2048,3,128]{2,1,0:T(4,128)(2,1)S(1)} fusion(bf16[3,3072,128]{2,0,1:T(4,128)(2,1)} %bitcast.118, s32[2048]{0:T(1024)S(1)} %broadcast_clamp_fusion.2), kind=kCustom, calls=%fused_computation.5 | custom fusion | bytes 3153920 | tf_op jit(solution)/shard_map/gather | solution.py:209
  293.8 1.4 copy.49
  295.2 35.5 %all-to-all-done.3 = bf16[1,16,192,512]{3,2,0,1:T(8,128)(2,1)} async-done(((bf16[1,16,192,512]{3,2,0,1:T(8,128)(2,1)}), bf16[1,16,192,512]{3,2,0,1:T(8,128)(2,1)}, u32[]{:S(2)}, u32[]{:S(2)}) %all-to-all-start.3) | async-done | bytes 3145760 | tf_op jit(solution)/shard_map/all_to_all | solution.py:193
  330.7 11.7 %gather_fusion.4 = bf16[2048,512]{1,0:T(8,128)(2,1)} fusion(bf16[3072,512]{1,0:T(8,128)(2,1)} %bitcast.25, s32[2048]{0:T(1024)S(1)} %broadcast_clamp_fusion.2), kind=kCustom, calls=%fused_computation.4 | custom fusion | bytes 4202496 | tf_op jit(solution)/shard_map/gather | solution.py:208
  (71 shorter events, 0.3 us)
Async XLA Ops:
  0.6 72.6 %copy-start = (bf16[1024,9,128]{2,0,1:T(8,128)(2,1)S(1)}, bf16[1024,9,128]{2,0,1:T(8,128)(2,1)}, u32[]{:S(2)}) copy-start(bf16[1024,9,128]{2,0,1:T(8,128)(2,1)} %param.17) | copy-start | bytes 7077892
  3.2 120.1 %collective-permute-start.1 = (bf16[1,1,1,256,128]{4,3,2,1,0:T(8,128)(2,1)S(1)}, bf16[1,1,1,256,128]{4,3,2,1,0:T(8,128)(2,1)S(1)}, u32[]{:S(2)}, u32[]{:S(2)}) collective-permute-start(bf16[1,1,1,256,128]{4,3,2,1,0:T(8,128)(2,1)S(1)} %bitcast.125), channel_id=1, source_target_pairs={{16,0},{0,16},{17,1},{1,17},{18,2},{2,18},{19,3},{3,19},{20,4},{4,... | collective-permute-start | bytes 196616 | tf_op jit(solution)/shard_map/ppermute | solution.py:21
  6.2 117.0 %collective-permute-start = (bf16[1,1,1,256,128]{4,3,2,1,0:T(8,128)(2,1)S(1)}, bf16[1,1,1,256,128]{4,3,2,1,0:T(8,128)(2,1)}, u32[]{:S(2)}, u32[]{:S(2)}) collective-permute-start(bf16[1,1,1,256,128]{4,3,2,1,0:T(8,128)(2,1)S(1)} %bitcast.126), channel_id=1, source_target_pairs={{0,16},{16,0},{1,17},{17,1},{2,18},{18,2},{3,19},{19,3},{4,20},{20... | collective-permute-start | bytes 196616 | tf_op jit(solution)/shard_map/ppermute | solution.py:20
  6.3 1.7 copy-start.14
  6.3 2.4 copy-start.15
  6.3 17.6 %copy-start.19 = (f32[3,128]{1,0:T(4,128)S(1)}, f32[3,128]{1,0:T(4,128)}, u32[]{:S(2)}) copy-start(f32[3,128]{1,0:T(4,128)} %param.30) | copy-start | bytes 4612
  6.3 27.6 %copy-start.11 = (f32[3,2048]{1,0:T(4,128)S(1)}, f32[3,2048]{1,0:T(4,128)}, u32[]{:S(2)}) copy-start(f32[3,2048]{1,0:T(4,128)} %param.19) | copy-start | bytes 73732
  8.1 37.0 %copy-start.12 = (s32[2048,1]{0,1:T(1,128)}, s32[2048,1]{0,1:T(1,128)S(1)}, u32[]{:S(2)}) copy-start(s32[2048,1]{0,1:T(1,128)S(1)} %compare_select_fusion.1) | copy-start | bytes 24580
  17.5 27.6 %all-to-all-start = ((s32[1,16,192]{2,0,1:T(1,128)}), s32[1,16,192]{2,0,1:T(1,128)S(1)}, u32[]{:S(2)}, u32[]{:S(2)}) async-start(s32[1,16,192]{2,0,1:T(1,128)} %reshape.245), calls=%async_computation | async-start | bytes 32768 | tf_op jit(solution)/shard_map/all_to_all | solution.py:150
  35.3 17.2 %copy-start.2 = (bf16[1024,128]{1,0:T(8,128)(2,1)S(1)}, bf16[1024,128]{1,0:T(8,128)(2,1)}, u32[]{:S(2)}) copy-start(bf16[1024,128]{1,0:T(8,128)(2,1)} %param.16) | copy-start | bytes 786436
  45.1 18.0 %all-to-all-start.1 = ((s32[1,16,192]{2,0,1:T(1,128)}), s32[1,16,192]{2,0,1:T(1,128)}, u32[]{:S(2)}, u32[]{:S(2)}) async-start(s32[1,16,192]{2,0,1:T(1,128)} %reshape.247), calls=%async_computation.1 | async-start | bytes 32768 | tf_op jit(solution)/shard_map/all_to_all | solution.py:157
  51.3 0.6 copy-start.9
  63.1 62.6 %all-to-all-start.2 = ((f32[3,16,192]{2,0,1:T(4,128)}), f32[3,16,192]{2,0,1:T(4,128)}, u32[]{:S(2)}, u32[]{:S(2)}) async-start(f32[3,16,192]{2,0,1:T(4,128)} %copy.42), calls=%async_computation.2 | async-start | bytes 131072 | tf_op jit(solution)/shard_map/all_to_all | solution.py:164
  124.1 6.7 %collective-permute-start.3 = (bf16[3,1,1,256,128]{4,3,2,1,0:T(8,128)(2,1)S(1)}, bf16[3,1,1,256,128]{4,3,2,1,0:T(8,128)(2,1)S(1)}, u32[]{:S(2)}, u32[]{:S(2)}) collective-permute-start(bf16[3,1,1,256,128]{4,3,2,1,0:T(8,128)(2,1)S(1)} %pad_maximum_fusion.4), channel_id=1, source_target_pairs={{4,0},{8,4},{12,8},{0,12},{5,1},{9,5},{13,9},{1,13},{6,2},{10,6},{... | collective-permute-start | bytes 589832 | tf_op jit(solution)/shard_map/ppermute | solution.py:21
  125.8 6.2 %collective-permute-start.2 = (bf16[3,1,1,256,128]{4,3,2,1,0:T(8,128)(2,1)S(1)}, bf16[3,1,1,256,128]{4,3,2,1,0:T(8,128)(2,1)S(1)}, u32[]{:S(2)}, u32[]{:S(2)}) collective-permute-start(bf16[3,1,1,256,128]{4,3,2,1,0:T(8,128)(2,1)S(1)} %pad_maximum_fusion.4), channel_id=1, source_target_pairs={{0,4},{4,8},{8,12},{12,0},{1,5},{5,9},{9,13},{13,1},{2,6},{6,10},{... | collective-permute-start | bytes 589832 | tf_op jit(solution)/shard_map/ppermute | solution.py:20
  132.8 17.2 %collective-permute-start.5 = (bf16[3,3,1,256,128]{4,3,2,1,0:T(8,128)(2,1)S(1)}, bf16[3,3,1,256,128]{4,3,2,1,0:T(8,128)(2,1)S(1)}, u32[]{:S(2)}, u32[]{:S(2)}) collective-permute-start(bf16[3,3,1,256,128]{4,3,2,1,0:T(8,128)(2,1)S(1)} %pad_maximum_fusion.3), channel_id=1, source_target_pairs={{1,0},{2,1},{3,2},{0,3},{5,4},{6,5},{7,6},{4,7},{9,8},{10,9},{11,1... | collective-permute-start | bytes 1769480 | tf_op jit(solution)/shard_map/ppermute | solution.py:21
  136.3 25.6 %collective-permute-start.4 = (bf16[3,3,1,256,128]{4,3,2,1,0:T(8,128)(2,1)S(1)}, bf16[3,3,1,256,128]{4,3,2,1,0:T(8,128)(2,1)S(1)}, u32[]{:S(2)}, u32[]{:S(2)}) collective-permute-start(bf16[3,3,1,256,128]{4,3,2,1,0:T(8,128)(2,1)S(1)} %pad_maximum_fusion.3), channel_id=1, source_target_pairs={{0,1},{1,2},{2,3},{3,0},{4,5},{5,6},{6,7},{7,4},{8,9},{9,10},{10,1... | collective-permute-start | bytes 1769480 | tf_op jit(solution)/shard_map/ppermute | solution.py:20
  162.9 0.7 copy-start.10
  163.6 9.2 %copy-start.8 = (bf16[128,512]{1,0:T(8,128)(2,1)S(1)}, bf16[128,512]{1,0:T(8,128)(2,1)}, u32[]{:S(2)}) copy-start(bf16[128,512]{1,0:T(8,128)(2,1)} %param.25) | copy-start | bytes 393220
  172.8 1.0 copy-start.22
  172.8 1.0 copy-start.24
  173.8 6.5 %copy-start.20 = (bf16[512,512]{1,0:T(8,128)(2,1)S(1)}, bf16[512,512]{1,0:T(8,128)(2,1)}, u32[]{:S(2)}) copy-start(bf16[512,512]{1,0:T(8,128)(2,1)} %param.27) | copy-start | bytes 1572868
  173.8 11.1 %slice-start = ((s8[7077888]{0:T(1024)(128)(4,1)}), s8[2883584]{0:T(1024)(128)(4,1)S(1)}, s32[]{:S(2)}) async-start(s8[7077888]{0:T(1024)(128)(4,1)} %bitcast.115), calls=%async_computation.5 | async-start | bytes 5767168
  180.4 2.7 copy-start.7
  180.4 4.6 %slice-start.1 = ((s8[7077888]{0:T(1024)(128)(4,1)}), s8[4194304]{0:T(1024)(128)(4,1)S(1)}, s32[]{:S(2)}) async-start(s8[7077888]{0:T(1024)(128)(4,1)} %bitcast.115), calls=%async_computation.6 | async-start | bytes 8388608
  183.1 1.8 copy-start.4
  183.1 1.9 copy-start.16
  183.1 1.9 copy-start.17
  183.1 1.9 copy-start.18
  184.9 4.8 %copy-start.3 = (f32[3072,384]{1,0:T(8,128)}, f32[3072,384]{1,0:T(8,128)S(1)}, u32[]{:S(2)}) copy-start(f32[3072,384]{1,0:T(8,128)S(1)} %fusion.68) | copy-start | bytes 14155780
  194.4 59.8 %all-to-all-start.4 = ((bf16[3,16,192,128]{3,2,0,1:T(8,128)(2,1)}), bf16[3,16,192,128]{3,2,0,1:T(8,128)(2,1)S(1)}, u32[]{:S(2)}, u32[]{:S(2)}) async-start(bf16[3,16,192,128]{3,2,0,1:T(8,128)(2,1)} %pad_maximum_fusion), calls=%async_computation.4 | async-start | bytes 4718592 | tf_op jit(solution)/shard_map/all_to_all | solution.py:200
  199.3 5.8 %copy-start.5 = (bf16[3072,512]{1,0:T(8,128)(2,1)S(1)}, bf16[3072,512]{1,0:T(8,128)(2,1)}, u32[]{:S(2)}) copy-start(bf16[3072,512]{1,0:T(8,128)(2,1)} %copy-done.4) | copy-start | bytes 9437188
  199.3 5.8 %copy-start.6 = (bf16[3072,128]{1,0:T(8,128)(2,1)S(1)}, bf16[3072,128]{1,0:T(8,128)(2,1)}, u32[]{:S(2)}) copy-start(bf16[3072,128]{1,0:T(8,128)(2,1)} %get-tuple-element.19) | copy-start | bytes 2359300
  199.3 5.8 %copy-start.21 = (bf16[384,512]{1,0:T(8,128)(2,1)S(1)}, bf16[384,512]{1,0:T(8,128)(2,1)}, u32[]{:S(2)}) copy-start(bf16[384,512]{1,0:T(8,128)(2,1)} %param.29) | copy-start | bytes 1179652
  199.3 5.8 %copy-start.23 = (f32[512]{0:T(512)S(1)}, f32[512]{0:T(512)}, u32[]{:S(2)}) copy-start(f32[512]{0:T(512)} %param.31) | copy-start | bytes 6148
  254.2 4.6 %copy-start.13 = (s32[2048,1]{0,1:T(1,128)S(1)}, s32[2048,1]{0,1:T(1,128)}, u32[]{:S(2)}) copy-start(s32[2048,1]{0,1:T(1,128)} %copy-done.12) | copy-start | bytes 24580
  254.2 76.4 %all-to-all-start.3 = ((bf16[1,16,192,512]{3,2,0,1:T(8,128)(2,1)}), bf16[1,16,192,512]{3,2,0,1:T(8,128)(2,1)}, u32[]{:S(2)}, u32[]{:S(2)}) async-start(bf16[1,16,192,512]{3,2,0,1:T(8,128)(2,1)} %bitcast.124), calls=%async_computation.3 | async-start | bytes 6291456 | tf_op jit(solution)/shard_map/all_to_all | solution.py:193
  330.7 11.7 %copy-start.1 = (bf16[1024,9,128]{2,0,1:T(8,128)(2,1)S(1)}, bf16[1024,9,128]{2,0,1:T(8,128)(2,1)}, u32[]{:S(2)}) copy-start(bf16[1024,9,128]{2,0,1:T(8,128)(2,1)} %param.17) | copy-start | bytes 7077892
where the time goes:
time: 344 us; the launch traced here: 342 us
  local copies, waits for them, and re-layouts  126 us (37%)
  waiting for transfers between devices  109 us (32%)
  other arithmetic  46.2 us (13%)
  starting transfers between devices  36.2 us (11%)
  matrix products  23.4 us (7%)
    gather x1, local copies, waits for them, and re-layouts, local(): atom_env[center_rows]  45.3 us
    all_to_all x1, waiting for transfers between devices, local(): lax.all_to_all(vector_far.reshape(3, owners, capacity, channels), ('gy',...  43.9 us
    all_to_all x1, waiting for transfers between devices, local(): lax.all_to_all(latent_far.reshape(1, owners, capacity, -1), ('gy', 'gz'),...  35.5 us
    scatter-add x1, other arithmetic, local(): jax.ops.segment_sum(energy_far, center_rows, num_segments=atoms_here)  22.5 us
    ppermute x3, waiting for transfers between devices, with_halo(): after = lax.ppermute(leading, axis, down)  16.8 us
    ppermute x3, waiting for transfers between devices, with_halo(): before = lax.ppermute(last, axis, up)  12.9 us
    gather x1, local copies, waits for them, and re-layouts, local(): latent_out = back_latent.reshape(owners * capacity, -1)[slot]  11.7 us
    gather x1, local copies, waits for them, and re-layouts, local(): atom_feat[center_rows]  10.6 us
  transfers between devices with their start and end apart: 11, of which 6 were waited for; matrix products, arithmetic and copies ran while one was open for 43% of the time, Pallas kernels for 0%

commit v1 on v0

v1 whole, which is shorter than its diff:
```python
import functools

import jax
import jax.numpy as jnp
from jax import lax
from jax.experimental import pallas as pl
from jax.experimental.pallas import tpu as pltpu
from jax.sharding import PartitionSpec as P

cutoff = 6.0
root_two = 2.0**0.5
root_three = 3.0**0.5
root_five = 5.0**0.5
root_fifteen = 15.0**0.5
f32 = jnp.float32
bf16 = jnp.bfloat16
LANES = 128
NT = (((1,), (1,)), ((), ()))


def split3(v):
    high = v.astype(bf16).astype(f32)
    rest = v - high
    middle = rest.astype(bf16).astype(f32)
    return (high, middle, rest - middle)


def route_kernel(owners, cap, count_ref, owner_ref, center_ref, vec_ref, rows_ref, request_ref):
    slots = owner_ref.shape[1]
    padded = request_ref.shape[2]
    owner = owner_ref[...]
    center = center_ref[...]
    member = owner == lax.broadcasted_iota(jnp.int32, (owners, slots), 0)
    member = jnp.where(member, 1.0, 0.0)
    step = 256
    before = lax.broadcasted_iota(jnp.int32, (step, step), 0) < lax.broadcasted_iota(
        jnp.int32, (step, step), 1
    )
    before = jnp.where(before, 1.0, 0.0).astype(bf16)
    seen = jnp.zeros((owners, 1), f32)
    ranks = []
    for start in range(0, slots, step):
        part = member[:, start : start + step]
        earlier = jnp.dot(part.astype(bf16), before, preferred_element_type=f32) + seen
        ranks.append(jnp.sum(part * earlier, axis=0, keepdims=True))
        seen = seen + jnp.sum(part, axis=1, keepdims=True)
    rank = jnp.concatenate(ranks, axis=1)
    position = lax.broadcasted_iota(jnp.int32, (1, slots), 1)
    live = jnp.where(position < count_ref[0], 1.0, 0.0)
    vec = vec_ref[...]
    length = jnp.sqrt(jnp.sum(vec * vec, axis=0, keepdims=True))
    unit = vec / jnp.maximum(length, 1.0)
    rows_ref[0:3, :] = root_three * unit
    rows_ref[3:4, :] = live
    rows_ref[4:5, :] = owner.astype(f32) * cap + rank
    rows_ref[5:6, :] = owner.astype(f32)
    rows_ref[6:7, :] = center.astype(f32)
    rows_ref[7:8, :] = length
    code = center + 1
    values = [(code // 256).astype(f32), (code % 256).astype(f32)]
    for m in range(3):
        values.extend(split3(vec[m : m + 1, :]))
    listed = member * live
    left = jnp.concatenate([(listed * v).astype(bf16) for v in values], axis=0)
    place = rank.astype(jnp.int32) == lax.broadcasted_iota(jnp.int32, (padded, slots), 0)
    place = jnp.where(place, 1.0, 0.0).astype(bf16)
    sent = lax.dot_general(left, place, NT, preferred_element_type=f32)
    at = lambda i: sent[i * owners : (i + 1) * owners, :]
    request_ref[:, 0, :] = 256.0 * at(0) + at(1)
    for m in range(3):
        request_ref[:, 1 + m, :] = at(2 + 3 * m) + at(3 + 3 * m) + at(4 + 3 * m)


def owner_kernel(cap, request_ref, env_ref, out_ref, table_ref):
    group = request_ref.shape[0]
    components, atoms, channels = env_ref.shape

    @pl.when(pl.program_id(0) == 0)
    def _():
        for m in range(components):
            table_ref[:, m * channels : (m + 1) * channels] = env_ref[m]

    masks = []
    weights = []
    for g in range(group):
        block = request_ref[g]
        code, vec = (block[0:1, :], block[1:4, :])
        length = jnp.sqrt(jnp.sum(vec * vec, axis=0, keepdims=True))
        unit = vec / jnp.maximum(length, 1.0)
        ux, uy, uz = (unit[0:1], unit[1:2], unit[2:3])
        rows = jnp.concatenate(
            [
                code,
                root_fifteen * ux * uy,
                root_fifteen * uy * uz,
                0.5 * root_five * (2.0 * uz * uz - ux * ux - uy * uy),
                root_fifteen * ux * uz,
                0.5 * root_fifteen * (ux * ux - uy * uy),
                jnp.zeros_like(code),
                jnp.zeros_like(code),
            ],
            axis=0,
        )
        columns = jnp.transpose(rows)[:cap]
        atom = lax.broadcasted_iota(jnp.int32, (cap, atoms), 1) + 1
        hit = columns[:, 0:1].astype(jnp.int32) == atom
        masks.append(jnp.where(hit, 1.0, 0.0).astype(bf16))
        weights.append(columns)
    pick = jnp.concatenate(masks, axis=0)
    weight = jnp.concatenate(weights, axis=0)
    found = jnp.dot(pick, table_ref[...], preferred_element_type=f32)
    keep = 4 * channels
    out_ref[:, :keep] = found[:, :keep].astype(bf16)
    total = weight[:, 1:2] * found[:, keep : keep + channels]
    for m in range(1, 5):
        start = keep + m * channels
        total = total + weight[:, 1 + m : 2 + m] * found[:, start : start + channels]
    out_ref[:, keep:] = total.astype(bf16)


def final_kernel(
    owners,
    rows_ref,
    env_ref,
    mixed_ref,
    latent_ref,
    scalar_ref,
    gain_ref,
    energy_ref,
    latent_out_ref,
    vector_out_ref,
    sums_ref,
):
    many = rows_ref.shape[1]
    places = env_ref.shape[0]
    channels = gain_ref.shape[1]
    atoms = sums_ref.shape[1]
    columns = jnp.transpose(rows_ref[...])
    slot = columns[:, 4:5].astype(jnp.int32)
    hit = slot == lax.broadcasted_iota(jnp.int32, (many, places), 1)
    pick = jnp.where(hit, 1.0, 0.0).astype(bf16)
    env = jnp.dot(pick, env_ref[...], preferred_element_type=f32)
    part = lambda i: env[:, i * channels : (i + 1) * channels]
    env_scalar, env_vector, tensor = (part(0), [part(1), part(2), part(3)], part(4))
    mixed = mixed_ref[...]
    scalar_part = mixed[:, :channels]
    vector_part = mixed[:, channels : 2 * channels]
    tensor_part = mixed[:, 2 * channels :]
    edge = [vector_part * columns[:, m : m + 1] for m in range(3)]
    vector_dot = edge[0] * env_vector[0] + edge[1] * env_vector[1] + edge[2] * env_vector[2]
    invariants = jnp.concatenate(
        [
            (scalar_part * env_scalar).astype(bf16),
            (vector_dot * (1.0 / root_three)).astype(bf16),
            (tensor_part * tensor * (1.0 / root_five)).astype(bf16),
        ],
        axis=1,
    )
    live = columns[:, 3:4] > 0.5
    cross = [
        edge[1] * env_vector[2] - edge[2] * env_vector[1],
        edge[2] * env_vector[0] - edge[0] * env_vector[2],
        edge[0] * env_vector[1] - edge[1] * env_vector[0],
    ]
    gain = gain_ref[...]
    for m in range(3):
        value = (
            gain[0:1] * scalar_part * env_vector[m]
            + gain[1:2] * edge[m] * env_scalar
            + (gain[2:3] * (1.0 / root_two)) * cross[m]
        )
        vector_out_ref[m] = jnp.where(live, value, 0.0).astype(bf16)
    update = jnp.dot(invariants, scalar_ref[...], preferred_element_type=f32)
    update = update * jax.nn.sigmoid(update)
    latent = jnp.where(live, latent_ref[...].astype(f32) + update, 0.0).astype(bf16)
    latent_out_ref[...] = latent
    energy = jnp.sum(latent.astype(f32) * energy_ref[...], axis=1, keepdims=True)
    lane = lax.broadcasted_iota(jnp.int32, (many, LANES), 1)
    owner = columns[:, 5:6].astype(jnp.int32)
    spread = jnp.zeros((many, LANES), f32)
    for i, piece in enumerate(split3(energy)):
        spread = spread + jnp.where(lane == owner + i * owners, piece, 0.0)
    spread = jnp.transpose(spread).astype(bf16)
    center = columns[:, 6:7].astype(jnp.int32)
    of_atom = center == lax.broadcasted_iota(jnp.int32, (many, atoms), 1)
    of_atom = jnp.where(of_atom, 1.0, 0.0).astype(bf16)
    sums = jnp.dot(spread, of_atom, preferred_element_type=f32)
    sums = sums[:owners] + sums[owners : 2 * owners] + sums[2 * owners : 3 * owners]

    @pl.when(pl.program_id(0) == 0)
    def _():
        sums_ref[...] = sums

    @pl.when(pl.program_id(0) > 0)
    def _():
        sums_ref[...] = sums_ref[...] + sums


def whole(shape):
    return pl.BlockSpec(shape, lambda *_: (0,) * len(shape))


def swap(x, axis, bit):
    return lax.ppermute(x, axis, [(i, i ^ bit) for i in range(lax.axis_size(axis))])


def local(
    atom_feat,
    atom_env,
    export_index,
    pair_vec,
    pair_center,
    pair_owner,
    pair_neigh,
    pair_count,
    center_proj,
    neighbour_proj,
    radial_proj,
    hidden_proj,
    split_proj,
    scalar_proj,
    path_gain,
    energy_proj,
):
    atoms, channels = atom_feat.shape
    slots = pair_center.shape[0]
    exports = export_index.shape[0]
    latent_width = hidden_proj.shape[1]
    nx, ny, nz = (lax.axis_size("gx"), lax.axis_size("gy"), lax.axis_size("gz"))
    owners = ny * nz
    cap = 3 * slots // (2 * owners)
    padded = -(-cap // LANES) * LANES
    components = atom_env.shape[1]

    exported = atom_feat[export_index]
    up = [(i, (i + 1) % nx) for i in range(nx)]
    down = [(j, i) for i, j in up]
    parts = [atom_feat, exported, lax.ppermute(exported, "gx", up)]
    if nx > 2:
        parts.append(lax.ppermute(exported, "gx", down))
    block = jnp.concatenate(parts, axis=0)
    block_rows = block.shape[0]
    table = jnp.stack([block] + [swap(block, "gz", k) for k in range(1, nz)])
    bit = ny // 2
    while bit:
        table = jnp.stack([table, swap(table, "gy", bit)])
        bit //= 2
    bits = ny.bit_length() - 1
    table = table.reshape(-1, channels)

    rows, request = pl.pallas_call(
        functools.partial(route_kernel, owners, cap),
        out_shape=(
            jax.ShapeDtypeStruct((8, slots), f32),
            jax.ShapeDtypeStruct((owners, 4, padded), f32),
        ),
        in_specs=[pl.BlockSpec(memory_space=pltpu.SMEM)]
        + [pl.BlockSpec(memory_space=pltpu.VMEM)] * 3,
        out_specs=[pl.BlockSpec(memory_space=pltpu.VMEM)] * 2,
        name="route",
    )(pair_count, pair_owner.reshape(1, slots), pair_center.reshape(1, slots), pair_vec)
    request = lax.all_to_all(request, ("gy", "gz"), split_axis=0, concat_axis=0, tiled=True)

    group = min(4, owners)
    env = jnp.transpose(atom_env, (1, 0, 2))
    sent = pl.pallas_call(
        functools.partial(owner_kernel, cap),
        grid=(owners // group,),
        out_shape=jax.ShapeDtypeStruct((owners * cap, 5 * channels), bf16),
        in_specs=[
            pl.BlockSpec((group, 4, padded), lambda i: (i, 0, 0)),
            whole((components, atoms, channels)),
        ],
        out_specs=pl.BlockSpec((group * cap, 5 * channels), lambda i: (i, 0)),
        scratch_shapes=[pltpu.VMEM((atoms, components * channels), bf16)],
        compiler_params=pltpu.CompilerParams(dimension_semantics=("arbitrary",)),
        name="owner",
    )(request, env)
    received = lax.all_to_all(
        sent.reshape(owners, cap, 5 * channels),
        ("gy", "gz"),
        split_axis=0,
        concat_axis=0,
        tiled=True,
    ).reshape(owners * cap, 5 * channels)

    owner = pair_owner[:, 0]
    oy, oz = (owner // nz, owner % nz)
    my_y, my_z = (lax.axis_index("gy"), lax.axis_index("gz"))

    def place(y, z):
        dy, dz = (y ^ my_y, z ^ my_z)
        flipped = jnp.zeros_like(dy)
        for b in range(bits):
            flipped = flipped | (((dy >> b) & 1) << (bits - 1 - b))
        return (flipped * nz + dz) * block_rows

    center_at = place(oy, oz) + pair_center
    k = jnp.maximum(pair_neigh - atoms, 0)
    cell, member = (k // exports, k % exports)
    dx, dy, dz = (cell // 9 - 1, cell // 3 % 3 - 1, cell % 3 - 1)
    sy, sz = ((oy + dy) % ny, (oz + dz) % nz)
    if nx > 2:
        which = jnp.where(dx == 0, 0, jnp.where(dx < 0, 1, 2))
    else:
        which = jnp.where(dx == 0, 0, 1)
    halo_at = place(sy, sz) + atoms + which * exports + member
    neighbour_at = jnp.where(pair_neigh < atoms, place(oy, oz) + pair_neigh, halo_at)
    pair_feat = jnp.concatenate([table[center_at], table[neighbour_at]], axis=1)
    length = rows[7]
    basis = radial_proj.shape[0]
    spacing = cutoff / (basis - 1)
    centres = jnp.arange(basis).astype(f32) * spacing
    radial = jnp.exp(-jnp.square((length[:, None] - centres[None, :]) / spacing))
    both = jnp.concatenate([center_proj, neighbour_proj], axis=0)
    before = jnp.dot(pair_feat, both, preferred_element_type=f32)
    before = before + jnp.dot(radial, radial_proj.astype(f32), precision=lax.Precision.HIGHEST)
    hidden = jax.nn.silu(before).astype(bf16)
    latent = jax.nn.silu(jnp.dot(hidden, hidden_proj, preferred_element_type=f32)).astype(bf16)
    mixed = jnp.dot(latent, split_proj, preferred_element_type=f32)

    many = min(512, slots)
    latent_out, vector_out, sums = pl.pallas_call(
        functools.partial(final_kernel, owners),
        grid=(slots // many,),
        out_shape=(
            jax.ShapeDtypeStruct((slots, latent_width), bf16),
            jax.ShapeDtypeStruct((3, slots, channels), bf16),
            jax.ShapeDtypeStruct((owners, atoms), f32),
        ),
        in_specs=[
            pl.BlockSpec((8, many), lambda i: (0, i)),
            whole((owners * cap, 5 * channels)),
            pl.BlockSpec((many, 3 * channels), lambda i: (i, 0)),
            pl.BlockSpec((many, latent_width), lambda i: (i, 0)),
            whole(scalar_proj.shape),
            whole(path_gain.shape),
            whole((1, latent_width)),
        ],
        out_specs=(
            pl.BlockSpec((many, latent_width), lambda i: (i, 0)),
            pl.BlockSpec((3, many, channels), lambda i: (0, i, 0)),
            whole((owners, atoms)),
        ),
        compiler_params=pltpu.CompilerParams(dimension_semantics=("arbitrary",)),
        name="final",
    )(rows, received, mixed, latent, scalar_proj, path_gain, energy_proj.reshape(1, latent_width))
    sums = lax.all_to_all(sums, ("gy", "gz"), split_axis=0, concat_axis=0, tiled=True)
    return (latent_out, vector_out, jnp.sum(sums, axis=0))


def solution(mesh):
    placed = (
        P(("gx", "gy", "gz"), None),
        P(("gx", "gy", "gz"), None, None),
        P(("gx", "gy", "gz")),
        P(None, ("gx", "gy", "gz")),
        P(("gx", "gy", "gz")),
        P(("gx", "gy", "gz"), None),
        P(("gx", "gy", "gz")),
        P(("gx", "gy", "gz")),
        P(),
        P(),
        P(),
        P(),
        P(),
        P(),
        P(),
        P(),
    )
    return jax.shard_map(
        local,
        mesh=mesh,
        in_specs=placed,
        out_specs=(
            P(("gx", "gy", "gz"), None),
            P(None, ("gx", "gy", "gz"), None),
            P(("gx", "gy", "gz")),
        ),
        check_vma=False,
    )
```

time: 344 us -> 224 us (0.65)
  local copies, waits for them, and re-layouts: 126 us -> 22.9 us
  blocking collectives: 0 us -> 41.9 us
  Pallas kernels: 0 us -> 37.7 us
  other arithmetic: 46.2 us -> 13.4 us
  waiting for transfers between devices: 109 us -> 83.1 us
  starting transfers between devices: 36.2 us -> 14.2 us
  matrix products: 23.4 us -> 8.29 us
    gather x5 -> x2, local copies, waits for them, and re-layouts: 85.5 us -> 18.4 us  [local(): pair_feat = jnp.concatenate([table[center_at], table[neighbour_at]], axis=1)]
    all_to_all x0 -> x2, blocking collectives: none -> 41.9 us  [the longest x1 32.1 us: local(): lax.all_to_all(request, ('gy', 'gz'), split_axis=0, concat_axis=0, tiled=...]
    pallas_call x0 -> x3, Pallas kernels: none -> 37.7 us  [the longest x1 21.9 us: local(): pl.pallas_call(functools.partial(final_kernel, owners), grid=(slots // ma...]
    all_to_all x5 -> x1, waiting for transfers between devices: 79.4 us -> 45.1 us  [local(): lax.all_to_all(sent.reshape(owners, cap, 5 * channels), ('gy', 'gz'), spl...]
    scatter x3 -> x0, local copies, waits for them, and re-layouts: 23.4 us -> none  [the longest x1 8.22 us: local(): jnp.zeros((owners * capacity,), jnp.int32).at[slot].set(pair_neigh)]
    all_to_all x5 -> x1, starting transfers between devices: 28 us -> 4.71 us  [local(): lax.all_to_all(sent.reshape(owners, cap, 5 * channels), ('gy', 'gz'), spl...]
    scatter-add x1 -> x0, other arithmetic: 22.5 us -> none  [local(): jax.ops.segment_sum(energy_far, center_rows, num_segments=atoms_here)]
    dot_general x7 -> x4, matrix products: 23.4 us -> 8.29 us  [the longest x1 2.9 us: local(): mixed = jnp.dot(latent, split_proj, preferred_element_type=f32)]
  transfers between devices with their start and end apart: 11 -> 7, of which waited for: 6 -> 5; matrix products, arithmetic and copies ran while one was open for 43% -> 18% of each run, Pallas kernels for 0% -> 7%
where the time goes in v1:
time: 224 us; the launch traced here: 223 us
  waiting for transfers between devices  83.1 us (37%)
  blocking collectives  41.9 us (19%)
  Pallas kernels  37.7 us (17%)
  local copies, waits for them, and re-layouts  22.9 us (10%)
  starting transfers between devices  14.2 us (6%)
  other arithmetic  13.4 us (6%)
  matrix products  8.29 us (4%)
    all_to_all x1, waiting for transfers between devices, local(): lax.all_to_all(sent.reshape(owners, cap, 5 * channels), ('gy', 'gz'), spl...  45.1 us
    ppermute x5, waiting for transfers between devices, swap(): lax.ppermute(x, axis, [(i, i ^ bit) for i in range(lax.axis_size(axis))])  36.7 us
    all_to_all x1, blocking collectives, local(): lax.all_to_all(request, ('gy', 'gz'), split_axis=0, concat_axis=0, tiled=...  32.1 us
    pallas_call x1, Pallas kernels, local(): pl.pallas_call(functools.partial(final_kernel, owners), grid=(slots // ma...  21.9 us
    gather x2, local copies, waits for them, and re-layouts, local(): pair_feat = jnp.concatenate([table[center_at], table[neighbour_at]], axis=1)  18.4 us
    pallas_call x1, Pallas kernels, local(): pl.pallas_call(functools.partial(owner_kernel, cap), grid=(owners // grou...  13.6 us
    another operation x3, other arithmetic, local(): table = jnp.stack([table, swap(table, 'gy', bit)])  11.9 us
    all_to_all x1, blocking collectives, local(): lax.all_to_all(sums, ('gy', 'gz'), split_axis=0, concat_axis=0, tiled=True)  9.81 us
  transfers between devices with their start and end apart: 7, of which 5 were waited for; matrix products, arithmetic and copies ran while one was open for 18% of the time, Pallas kernels for 7%

profile of v1, /device:TPU:0, one launch (start us, length us, event | category | flops | bytes accessed | tf_op | source)
XLA Modules:
  0.0 222.9 jit_solution(6517151928330558304)
XLA Ops:
  0.6 0.0 copy-start
  0.6 0.7 compare_select_fusion.2
  1.4 1.7 gather_fusion
  3.1 3.0 %collective-permute-start = (bf16[256,128]{1,0:T(8,128)(2,1)S(1)}, bf16[256,128]{1,0:T(8,128)(2,1)S(1)}, u32[]{:S(2)}, u32[]{:S(2)}) collective-permute-start(bf16[256,128]{1,0:T(8,128)(2,1)S(1)} %gather_fusion), channel_id=1, source_target_pairs={{0,16},{16,0},{1,17},{17,1},{2,18},{18,2},{3,19},{19,3},{4,20},{20... | collective-permute-start | bytes 196616 | tf_op jit(solution)/shard_map/ppermute | solution.py:238
  6.1 1.0 constant_dynamic-update-slice_fusion.2
  7.1 1.3 collective-permute-done
  8.4 4.2 %collective-permute-start.3 = (bf16[1536,128]{1,0:T(8,128)(2,1)S(1)}, bf16[1536,128]{1,0:T(8,128)(2,1)S(1)}, u32[]{:S(2)}, u32[]{:S(2)}) collective-permute-start(bf16[1536,128]{1,0:T(8,128)(2,1)S(1)} %constant_dynamic-update-slice_fusion), channel_id=1, source_target_pairs={{0,3},{1,2},{2,1},{3,0},{4,7},{5,6},{6,5},{7,4},{8,11},{9,10},{10,... | collective-permute-start | bytes 1179656 | tf_op jit(solution)/shard_map/ppermute | solution.py:204
  12.6 0.0 collective-permute-start.2
  12.6 0.6 collective-permute-start.1
  13.2 9.4 %collective-permute-done.3 = bf16[1536,128]{1,0:T(8,128)(2,1)S(1)} collective-permute-done((bf16[1536,128]{1,0:T(8,128)(2,1)S(1)}, bf16[1536,128]{1,0:T(8,128)(2,1)S(1)}, u32[]{:S(2)}, u32[]{:S(2)}) %collective-permute-start.3) | collective-permute-done | bytes 393248 | tf_op jit(solution)/shard_map/ppermute | solution.py:204
  22.7 22.3 %collective-permute-done.2 = bf16[1536,128]{1,0:T(8,128)(2,1)S(1)} collective-permute-done((bf16[1536,128]{1,0:T(8,128)(2,1)S(1)}, bf16[1536,128]{1,0:T(8,128)(2,1)S(1)}, u32[]{:S(2)}, u32[]{:S(2)}) %collective-permute-start.2) | collective-permute-done | bytes 393248 | tf_op jit(solution)/shard_map/ppermute | solution.py:204
  45.0 0.0 collective-permute-done.1
  45.0 1.4 fusion.42
  46.4 1.5 collective-permute-start.4
  48.6 2.2 route.1
  50.7 32.1 %all_to_all.19.request_ref = f32[16,4,256]{2,1,0:T(4,128)} all-to-all(f32[16,4,256]{2,1,0:T(4,128)} %get-tuple-element.9), channel_id=1, replica_groups=mesh['gx'=2,'gy'=4,'gz'=4] {'gy','gz'}, dimensions={0} | all-to-all | bytes 131072 | tf_op jit(solution)/shard_map/all_to_all | solution.py:262
  82.8 13.6 %owner.1 = bf16[3072,640]{1,0:T(8,128)(2,1)} custom-call(f32[16,4,256]{2,1,0:T(4,128)} %all_to_all.19.request_ref, bf16[9,1024,128]{2,1,0:T(8,128)(2,1)} %bitcast.28), custom_call_target="tpu_custom_call" | custom-call | tf_op jit(solution)/shard_map/owner/pallas_call | solution.py:266
  96.5 4.7 %all-to-all-start.1 = ((bf16[16,192,640]{2,1,0:T(8,128)(2,1)}), bf16[16,192,640]{2,1,0:T(8,128)(2,1)}, u32[]{:S(2)}, u32[]{:S(2)}) async-start(bf16[16,192,640]{2,1,0:T(8,128)(2,1)} %bitcast.27), calls=%async_computation.1 | async-start | bytes 7864320 | tf_op jit(solution)/shard_map/all_to_all | solution.py:279
  101.2 0.0 collective-permute-done.4
  101.2 0.0 copy-start.5
  101.2 0.0 copy-start.6
  101.2 0.0 copy-start.7
  101.2 4.4 %fusion.41 = (bf16[1,2,4,1536,128]{4,3,2,1,0:T(8,128)(2,1)}, bf16[2,4,1536,128]{3,2,1,0:T(8,128)(2,1)}) fusion(bf16[1,4,1536,128]{3,2,1,0:T(8,128)(2,1)} %bitcast.10, bf16[1,4,1536,128]{3,2,1,0:T(8,128)(2,1)S(1)} %get-tuple-element.15), kind=kLoop, calls=%fused_computation.81 | loop fusion | flops 1572864 | bytes 9437184 | tf_op jit(solution)/shard_map/stack | solution.py:246
  105.6 0.1 collective-permute-start.5
  105.7 0.8 slice.3
  106.6 0.0 copy-done.5
  106.6 0.0 copy-done.6
  106.6 0.0 copy-done.7
  106.6 0.1 fusion.32
  106.7 5.0 %collective-permute-done.5 = bf16[2,4,1536,128]{3,2,1,0:T(8,128)(2,1)} collective-permute-done((bf16[2,4,1536,128]{3,2,1,0:T(8,128)(2,1)}, bf16[2,4,1536,128]{3,2,1,0:T(8,128)(2,1)}, u32[]{:S(2)}, u32[]{:S(2)}) %collective-permute-start.5) | collective-permute-done | bytes 3145760 | tf_op jit(solution)/shard_map/ppermute | solution.py:204
  111.6 6.1 %pad_maximum_fusion = bf16[2,2,4,1536,128]{4,3,2,1,0:T(8,128)(2,1)} fusion(bf16[1,2,4,1536,128]{4,3,2,1,0:T(8,128)(2,1)} %bitcast.12, bf16[1,2,4,1536,128]{4,3,2,1,0:T(8,128)(2,1)} %get-tuple-element.13), kind=kLoop, calls=%fused_computation.3 | loop fusion | flops 3145728 | bytes 12582912 | tf_op jit(solution)/shard_map/stack | solution.py:246
  117.7 9.2 %gather_fusion.2 = bf16[2048,128]{1,0:T(8,128)(2,1)S(1)} fusion(bf16[24576,128]{1,0:T(8,128)(2,1)} %bitcast.25, s32[2048]{0:T(1024)S(1)} %get-tuple-element.18), kind=kCustom, calls=%fused_computation.2 | custom fusion | bytes 1056768 | tf_op jit(solution)/shard_map/gather | solution.py:309
  126.9 0.0 copy-start.3
  126.9 0.0 copy-start.4
  126.9 9.2 %gather_fusion.1 = bf16[2048,128]{1,0:T(8,128)(2,1)S(1)} fusion(bf16[24576,128]{1,0:T(8,128)(2,1)} %bitcast.26, s32[2048]{0:T(1024)S(1)} %get-tuple-element.17), kind=kCustom, calls=%fused_computation.1 | custom fusion | bytes 1056768 | tf_op jit(solution)/shard_map/gather | solution.py:309
  136.2 0.0 copy-done.3
  136.2 0.0 copy-done.4
  136.2 0.0 copy-start.8
  136.2 0.7 fusion
  136.9 0.0 copy-done.8
  136.9 2.9 %multiply_convert_fusion.1 = bf16[2048,512]{1,0:T(8,128)(2,1)S(1)} fusion(f32[2048,512]{1,0:T(8,128)S(1)} %fusion, bf16[8,512]{1,0:T(8,128)(2,1)S(1)} %copy-done.8, f32[8]{0:T(128)S(1)} %convert_multiply_fusion, f32[2048]{0:T(1024)S(1)} %bitcast.37), kind=kOutput, calls=%fused_computation.5 | convolution fusion | flops 107020288 | bytes 6307872 | tf_op jit(solution)/shard_map/dot_general | solution.py:317
  139.8 0.0 copy-done
  139.8 0.0 copy-start.2
  139.8 1.8 multiply_convert_fusion.latent_ref
  141.7 0.0 copy-done.2
  141.7 0.0 copy-start.1
  141.7 2.9 %fusion.43.mixed_ref = f32[2048,384]{1,0:T(8,128)} fusion(bf16[2048,512]{1,0:T(8,128)(2,1)S(1)} %multiply_convert_fusion.latent_ref, bf16[512,384]{1,0:T(8,128)(2,1)S(1)} %copy-done.2), kind=kOutput, calls=%fused_computation.83 | convolution fusion | flops 805306368 | bytes 5636096 | tf_op jit(solution)/shard_map/dot_general | solution.py:320
  144.6 0.0 copy-done.1
  144.6 45.1 %all-to-all-done.1 = bf16[16,192,640]{2,1,0:T(8,128)(2,1)} async-done(((bf16[16,192,640]{2,1,0:T(8,128)(2,1)}), bf16[16,192,640]{2,1,0:T(8,128)(2,1)}, u32[]{:S(2)}, u32[]{:S(2)}) %all-to-all-start.1) | async-done | bytes 3932192 | tf_op jit(solution)/shard_map/all_to_all | solution.py:279
  189.7 21.9 %final.1 = (bf16[2048,512]{1,0:T(8,128)(2,1)}, bf16[3,2048,128]{2,1,0:T(8,128)(2,1)}, f32[16,1024]{1,0:T(8,128)}) custom-call(f32[8,2048]{1,0:T(8,128)} %get-tuple-element.8.rows_ref, bf16[3072,640]{1,0:T(8,128)(2,1)} %bitcast.4.env_ref, f32[2048,384]{1,0:T(8,128)} %fusion.43.mixed_ref, bf16[2048,512]{1,0:T(8,128)(2,1)} %copy-done.1, ...), custom_call_target="tpu_custom_call" | custom-call | tf_op jit(solution)/shard_map/final/pallas_call | solution.py:323
  211.6 0.9 copy.20
  212.5 9.8 %all_to_all.20 = f32[16,1,1024]{2,1,0:T(1,128)S(1)} all-to-all(f32[16,1,1024]{2,1,0:T(1,128)S(1)} %copy.20), channel_id=1, replica_groups=mesh['gx'=2,'gy'=4,'gz'=4] {'gy','gz'}, dimensions={0} | all-to-all | bytes 131072 | tf_op jit(solution)/shard_map/all_to_all | solution.py:348
  222.3 0.6 reduce_sum.9
  (4 shorter events, 0.0 us)
Async XLA Ops:
  0.6 139.2 %copy-start = (bf16[512,512]{1,0:T(8,128)(2,1)S(1)}, bf16[512,512]{1,0:T(8,128)(2,1)}, u32[]{:S(2)}) copy-start(bf16[512,512]{1,0:T(8,128)(2,1)} %param.27) | copy-start | bytes 1572868
  3.1 5.3 %collective-permute-start = (bf16[256,128]{1,0:T(8,128)(2,1)S(1)}, bf16[256,128]{1,0:T(8,128)(2,1)S(1)}, u32[]{:S(2)}, u32[]{:S(2)}) collective-permute-start(bf16[256,128]{1,0:T(8,128)(2,1)S(1)} %gather_fusion), channel_id=1, source_target_pairs={{0,16},{16,0},{1,17},{17,1},{2,18},{18,2},{3,19},{19,3},{4,20},{20... | collective-permute-start | bytes 196616 | tf_op jit(solution)/shard_map/ppermute | solution.py:238
  8.4 14.3 %collective-permute-start.3 = (bf16[1536,128]{1,0:T(8,128)(2,1)S(1)}, bf16[1536,128]{1,0:T(8,128)(2,1)S(1)}, u32[]{:S(2)}, u32[]{:S(2)}) collective-permute-start(bf16[1536,128]{1,0:T(8,128)(2,1)S(1)} %constant_dynamic-update-slice_fusion), channel_id=1, source_target_pairs={{0,3},{1,2},{2,1},{3,0},{4,7},{5,6},{6,5},{7,4},{8,11},{9,10},{10,... | collective-permute-start | bytes 1179656 | tf_op jit(solution)/shard_map/ppermute | solution.py:204
  12.6 32.4 %collective-permute-start.2 = (bf16[1536,128]{1,0:T(8,128)(2,1)S(1)}, bf16[1536,128]{1,0:T(8,128)(2,1)S(1)}, u32[]{:S(2)}, u32[]{:S(2)}) collective-permute-start(bf16[1536,128]{1,0:T(8,128)(2,1)S(1)} %constant_dynamic-update-slice_fusion), channel_id=1, source_target_pairs={{0,2},{1,3},{2,0},{3,1},{4,6},{5,7},{6,4},{7,5},{8,10},{9,11},{10,... | collective-permute-start | bytes 1179656 | tf_op jit(solution)/shard_map/ppermute | solution.py:204
  12.6 32.4 %collective-permute-start.1 = (bf16[1536,128]{1,0:T(8,128)(2,1)S(1)}, bf16[1536,128]{1,0:T(8,128)(2,1)S(1)}, u32[]{:S(2)}, u32[]{:S(2)}) collective-permute-start(bf16[1536,128]{1,0:T(8,128)(2,1)S(1)} %constant_dynamic-update-slice_fusion), channel_id=1, source_target_pairs={{0,1},{1,0},{2,3},{3,2},{4,5},{5,4},{6,7},{7,6},{8,9},{9,8},{10,11... | collective-permute-start | bytes 1179656 | tf_op jit(solution)/shard_map/ppermute | solution.py:204
  46.4 54.8 %collective-permute-start.4 = (bf16[4,1536,128]{2,1,0:T(8,128)(2,1)}, bf16[4,1536,128]{2,1,0:T(8,128)(2,1)}, u32[]{:S(2)}, u32[]{:S(2)}) collective-permute-start(bf16[4,1536,128]{2,1,0:T(8,128)(2,1)} %get-tuple-element.16), channel_id=1, source_target_pairs={{0,8},{4,12},{8,0},{12,4},{1,9},{5,13},{9,1},{13,5},{2,10},{6,14},... | collective-permute-start | bytes 4718600 | tf_op jit(solution)/shard_map/ppermute | solution.py:204
  96.5 93.2 %all-to-all-start.1 = ((bf16[16,192,640]{2,1,0:T(8,128)(2,1)}), bf16[16,192,640]{2,1,0:T(8,128)(2,1)}, u32[]{:S(2)}, u32[]{:S(2)}) async-start(bf16[16,192,640]{2,1,0:T(8,128)(2,1)} %bitcast.27), calls=%async_computation.1 | async-start | bytes 7864320 | tf_op jit(solution)/shard_map/all_to_all | solution.py:279
  101.2 5.4 %copy-start.5 = (s32[2048,1]{0,1:T(1,128)S(1)}, s32[2048,1]{0,1:T(1,128)}, u32[]{:S(2)}) copy-start(s32[2048,1]{0,1:T(1,128)} %param.21) | copy-start | bytes 24580
  101.2 5.4 %copy-start.6 = (s32[2048]{0:T(1024)S(1)}, s32[2048]{0:T(1024)}, u32[]{:S(2)}) copy-start(s32[2048]{0:T(1024)} %param.20) | copy-start | bytes 24580
  101.2 5.4 %copy-start.7 = (s32[2048]{0:T(1024)S(1)}, s32[2048]{0:T(1024)}, u32[]{:S(2)}) copy-start(s32[2048]{0:T(1024)} %param.22) | copy-start | bytes 24580
  105.6 6.0 %collective-permute-start.5 = (bf16[2,4,1536,128]{3,2,1,0:T(8,128)(2,1)}, bf16[2,4,1536,128]{3,2,1,0:T(8,128)(2,1)}, u32[]{:S(2)}, u32[]{:S(2)}) collective-permute-start(bf16[2,4,1536,128]{3,2,1,0:T(8,128)(2,1)} %get-tuple-element.14), channel_id=1, source_target_pairs={{0,4},{4,0},{8,12},{12,8},{1,5},{5,1},{9,13},{13,9},{2,6},{6,2},{1... | collective-permute-start | bytes 9437192 | tf_op jit(solution)/shard_map/ppermute | solution.py:204
  126.9 9.3 %copy-start.3 = (bf16[128,512]{1,0:T(8,128)(2,1)S(1)}, bf16[128,512]{1,0:T(8,128)(2,1)}, u32[]{:S(2)}) copy-start(bf16[128,512]{1,0:T(8,128)(2,1)} %param.25) | copy-start | bytes 393220
  126.9 9.3 %copy-start.4 = (bf16[128,512]{1,0:T(8,128)(2,1)S(1)}, bf16[128,512]{1,0:T(8,128)(2,1)}, u32[]{:S(2)}) copy-start(bf16[128,512]{1,0:T(8,128)(2,1)} %param.24) | copy-start | bytes 393220
  136.2 0.7 copy-start.8
  139.8 1.9 copy-start.2
  141.7 2.9 %copy-start.1 = (bf16[2048,512]{1,0:T(8,128)(2,1)}, bf16[2048,512]{1,0:T(8,128)(2,1)S(1)}, u32[]{:S(2)}) copy-start(bf16[2048,512]{1,0:T(8,128)(2,1)S(1)} %multiply_convert_fusion.latent_ref) | copy-start | bytes 6291460

commit v2 on v1

--- a/solution.py
+++ b/solution.py
@@ -6,6 +6,7 @@
 from jax.experimental import pallas as pl
 from jax.experimental.pallas import tpu as pltpu
 from jax.sharding import PartitionSpec as P
+
 
 cutoff = 6.0
 root_two = 2.0**0.5
@@ -15,6 +16,7 @@
 f32 = jnp.float32
 bf16 = jnp.bfloat16
 LANES = 128
+STEP = 256
 NT = (((1,), (1,)), ((), ()))
 
 
@@ -25,35 +27,55 @@
     return (high, middle, rest - middle)
 
 
-def route_kernel(owners, cap, count_ref, owner_ref, center_ref, vec_ref, rows_ref, request_ref):
+def route_kernel(
+    owners,
+    cap,
+    window,
+    count_ref,
+    owner_ref,
+    center_ref,
+    vec_ref,
+    export_ref,
+    rows_ref,
+    starts_ref,
+    request_ref,
+):
     slots = owner_ref.shape[1]
     padded = request_ref.shape[2]
     owner = owner_ref[...]
     center = center_ref[...]
     member = owner == lax.broadcasted_iota(jnp.int32, (owners, slots), 0)
     member = jnp.where(member, 1.0, 0.0)
-    step = 256
+    step = STEP
     before = lax.broadcasted_iota(jnp.int32, (step, step), 0) < lax.broadcasted_iota(
         jnp.int32, (step, step), 1
     )
     before = jnp.where(before, 1.0, 0.0).astype(bf16)
     seen = jnp.zeros((owners, 1), f32)
+    lane = lax.broadcasted_iota(jnp.int32, starts_ref.shape, 1)
+    starts = jnp.zeros(starts_ref.shape, f32)
     ranks = []
+    bases = []
     for start in range(0, slots, step):
         part = member[:, start : start + step]
         earlier = jnp.dot(part.astype(bf16), before, preferred_element_type=f32) + seen
         ranks.append(jnp.sum(part * earlier, axis=0, keepdims=True))
+        base = jnp.minimum(jnp.floor(seen * (1.0 / 16.0)) * 16.0, cap - window)
+        bases.append(jnp.sum(part * base, axis=0, keepdims=True))
         seen = seen + jnp.sum(part, axis=1, keepdims=True)
+        starts = jnp.where(lane == start // step + 1, seen, starts)
+    starts_ref[...] = starts.astype(jnp.int32)
     rank = jnp.concatenate(ranks, axis=1)
+    place_in = owner.astype(f32) * window + rank - jnp.concatenate(bases, axis=1)
     position = lax.broadcasted_iota(jnp.int32, (1, slots), 1)
     live = jnp.where(position < count_ref[0], 1.0, 0.0)
     vec = vec_ref[...]
     length = jnp.sqrt(jnp.sum(vec * vec, axis=0, keepdims=True))
     unit = vec / jnp.maximum(length, 1.0)
     rows_ref[0:3, :] = root_three * unit
-    rows_ref[3:4, :] = live
+    rows_ref[3:4, :] = place_in
     rows_ref[4:5, :] = owner.astype(f32) * cap + rank
-    rows_ref[5:6, :] = owner.astype(f32)
+    rows_ref[5:6, :] = jnp.where(live > 0.5, owner.astype(f32), -1.0)
     rows_ref[6:7, :] = center.astype(f32)
     rows_ref[7:8, :] = length
     code = center + 1
@@ -66,9 +88,23 @@
     place = jnp.where(place, 1.0, 0.0).astype(bf16)
     sent = lax.dot_general(left, place, NT, preferred_element_type=f32)
     at = lambda i: sent[i * owners : (i + 1) * owners, :]
-    request_ref[:, 0, :] = 256.0 * at(0) + at(1)
-    for m in range(3):
-        request_ref[:, 1 + m, :] = at(2 + 3 * m) + at(3 + 3 * m) + at(4 + 3 * m)
+    fields = [256.0 * at(0) + at(1)]
+    fields += [at(2 + 3 * m) + at(3 + 3 * m) + at(4 + 3 * m) for m in range(3)]
+    exports = export_ref.shape[1]
+    exported = export_ref[...].astype(f32)
+    free = padded - cap
+    if request_ref.shape[1] == 4:
+        lane = lax.broadcasted_iota(jnp.int32, (1, padded), 1)
+        rest = jnp.concatenate([exported] * (-(-padded // exports)), axis=1)[:, :padded]
+        for m in range(4):
+            shift = (cap - m * free) % exports
+            turned = pltpu.roll(jnp.broadcast_to(rest, (8, padded)), shift, 1)[:1]
+            fields[m] = jnp.where(lane >= cap, turned, fields[m])
+    for m in range(4):
+        request_ref[:, m, :] = fields[m]
+    for m in range(4, request_ref.shape[1]):
+        piece = exported[:, (m - 4) * padded : (m - 3) * padded]
+        request_ref[:, m, :] = jnp.broadcast_to(piece, (owners, padded))
 
 
 def owner_kernel(cap, request_ref, env_ref, out_ref, table_ref):
@@ -118,8 +154,53 @@
     out_ref[:, keep:] = total.astype(bf16)
 
 
+def latent_kernel(basis, block_rows, index_ref, lists_ref, rows_ref, *refs):
+    pieces = refs[:-8]
+    both_ref, radial_ref, hidden_ref, split_ref, latent_ref, mixed_ref = refs[-8:-2]
+    table_ref, feat_ref = refs[-2:]
+    many, _ = feat_ref.shape[1:]
+
+    @pl.when(pl.program_id(0) == 0)
+    def _():
+        for i, piece in enumerate(pieces):
+            table_ref[i * block_rows : (i + 1) * block_rows, :] = piece[...].astype(f32)
+
+    start = pl.program_id(0) * many
+    unroll = 16
+
+    def gather(i, carry):
+        at = pl.multiple_of(i * unroll, unroll)
+        read = (start + at) * 3
+        centers = [index_ref[read + 3 * j] for j in range(unroll)]
+        entries = [index_ref[read + 3 * j + 2] for j in range(unroll)]
+        neighbours = [index_ref[read + 3 * j + 1] + lists_ref[entries[j]] for j in range(unroll)]
+        for j in range(unroll):
+            feat_ref[0, pl.ds(at + j, 1), :] = table_ref[pl.ds(centers[j], 1), :]
+            feat_ref[1, pl.ds(at + j, 1), :] = table_ref[pl.ds(neighbours[j], 1), :]
+        return carry
+
+    lax.fori_loop(0, many // unroll, gather, 0)
+    spacing = cutoff / (basis - 1)
+    length = rows_ref[7:8, :]
+    centres = lax.broadcasted_iota(jnp.int32, (basis, many), 0).astype(f32) * spacing
+    scaled = (length - centres) / spacing
+    radial = jnp.concatenate(split3(jnp.exp(-(scaled * scaled))), axis=0)
+    radial = jnp.transpose(radial).astype(bf16)
+    feat = jnp.concatenate([feat_ref[0], feat_ref[1]], axis=1).astype(bf16)
+    before = jnp.dot(feat, both_ref[...], preferred_element_type=f32)
+    before = before + jnp.dot(radial, radial_ref[...], preferred_element_type=f32)
+    hidden = (before * jax.nn.sigmoid(before)).astype(bf16)
+    after = jnp.dot(hidden, hidden_ref[...], preferred_element_type=f32)
+    latent = (after * jax.nn.sigmoid(after)).astype(bf16)
+    latent_ref[...] = latent
+    mixed_ref[...] = jnp.dot(latent, split_ref[...], preferred_element_type=f32)
+
+
 def final_kernel(
     owners,
+    cap,
+    window,
+    starts_ref,
     rows_ref,
     env_ref,
     mixed_ref,
@@ -130,16 +211,43 @@
     latent_out_ref,
     vector_out_ref,
     sums_ref,
+    near_ref,
+    found_ref,
 ):
     many = rows_ref.shape[1]
     places = env_ref.shape[0]
     channels = gain_ref.shape[1]
     atoms = sums_ref.shape[1]
     columns = jnp.transpose(rows_ref[...])
-    slot = columns[:, 4:5].astype(jnp.int32)
-    hit = slot == lax.broadcasted_iota(jnp.int32, (many, places), 1)
-    pick = jnp.where(hit, 1.0, 0.0).astype(bf16)
-    env = jnp.dot(pick, env_ref[...], preferred_element_type=f32)
+    step = pl.program_id(0)
+
+    def pick(column, size):
+        hit = columns[:, column : column + 1].astype(jnp.int32) == lax.broadcasted_iota(
+            jnp.int32, (many, size), 1
+        )
+        return jnp.where(hit, 1.0, 0.0).astype(bf16)
+
+    fits = True
+    bases = []
+    for o in range(owners):
+        base = jnp.minimum(starts_ref[o, step] // 16 * 16, cap - window)
+        bases.append(base)
+        fits = fits & (starts_ref[o, step + 1] <= base + window)
+
+    @pl.when(fits)
+    def _():
+        for o in range(owners):
+            at = pl.multiple_of(o * cap + bases[o], 16)
+            near_ref[o * window : (o + 1) * window, :] = env_ref[pl.ds(at, window), :]
+        found_ref[...] = jnp.dot(
+            pick(3, owners * window), near_ref[...], preferred_element_type=f32
+        )
+
+    @pl.when(jnp.logical_not(fits))
+    def _():
+        found_ref[...] = jnp.dot(pick(4, places), env_ref[...], preferred_element_type=f32)
+
+    env = found_ref[...]
     part = lambda i: env[:, i * channels : (i + 1) * channels]
     env_scalar, env_vector, tensor = (part(0), [part(1), part(2), part(3)], part(4))
     mixed = mixed_ref[...]
@@ -156,7 +264,7 @@
         ],
         axis=1,
     )
-    live = columns[:, 3:4] > 0.5
+    live = columns[:, 5:6] >= 0.0
     cross = [
         edge[1] * env_vector[2] - edge[2] * env_vector[1],
         edge[2] * env_vector[0] - edge[0] * env_vector[2],
@@ -232,34 +340,41 @@
     padded = -(-cap // LANES) * LANES
     components = atom_env.shape[1]
 
+    fields = 4 if 4 * (padded - cap) >= exports else 4 + -(-exports // padded)
+    window = min(64, cap)
+    rows, starts, request = pl.pallas_call(
+        functools.partial(route_kernel, owners, cap, window),
+        out_shape=(
+            jax.ShapeDtypeStruct((8, slots), f32),
+            jax.ShapeDtypeStruct((owners, LANES), jnp.int32),
+            jax.ShapeDtypeStruct((owners, fields, padded), f32),
+        ),
+        in_specs=[pl.BlockSpec(memory_space=pltpu.SMEM)]
+        + [pl.BlockSpec(memory_space=pltpu.VMEM)] * 4,
+        out_specs=[pl.BlockSpec(memory_space=pltpu.VMEM)] * 3,
+        name="route",
+    )(
+        pair_count,
+        pair_owner.reshape(1, slots),
+        pair_center.reshape(1, slots),
+        pair_vec,
+        export_index.reshape(1, exports),
+    )
+    export_index, rows = lax.optimization_barrier((export_index, rows))
+    request = lax.all_to_all(request, ("gy", "gz"), split_axis=0, concat_axis=0, tiled=True)
+
     exported = atom_feat[export_index]
     up = [(i, (i + 1) % nx) for i in range(nx)]
     down = [(j, i) for i, j in up]
-    parts = [atom_feat, exported, lax.ppermute(exported, "gx", up)]
+    parts = [atom_feat, lax.ppermute(exported, "gx", up)]
     if nx > 2:
         parts.append(lax.ppermute(exported, "gx", down))
     block = jnp.concatenate(parts, axis=0)
     block_rows = block.shape[0]
-    table = jnp.stack([block] + [swap(block, "gz", k) for k in range(1, nz)])
-    bit = ny // 2
-    while bit:
-        table = jnp.stack([table, swap(table, "gy", bit)])
-        bit //= 2
-    bits = ny.bit_length() - 1
-    table = table.reshape(-1, channels)
-
-    rows, request = pl.pallas_call(
-        functools.partial(route_kernel, owners, cap),
-        out_shape=(
-            jax.ShapeDtypeStruct((8, slots), f32),
-            jax.ShapeDtypeStruct((owners, 4, padded), f32),
-        ),
-        in_specs=[pl.BlockSpec(memory_space=pltpu.SMEM)]
-        + [pl.BlockSpec(memory_space=pltpu.VMEM)] * 3,
-        out_specs=[pl.BlockSpec(memory_space=pltpu.VMEM)] * 2,
-        name="route",
-    )(pair_count, pair_owner.reshape(1, slots), pair_center.reshape(1, slots), pair_vec)
-    request = lax.all_to_all(request, ("gy", "gz"), split_axis=0, concat_axis=0, tiled=True)
+    block, request = lax.optimization_barrier((block, request))
+    pieces = {(0, 0): block}
+    for k in range(1, nz):
+        pieces[0, k] = swap(block, "gz", k)
 
     group = min(4, owners)
     env = jnp.transpose(atom_env, (1, 0, 2))
@@ -268,14 +383,24 @@
         grid=(owners // group,),
         out_shape=jax.ShapeDtypeStruct((owners * cap, 5 * channels), bf16),
         in_specs=[
-            pl.BlockSpec((group, 4, padded), lambda i: (i, 0, 0)),
+            pl.BlockSpec((group, fields, padded), lambda i: (i, 0, 0)),
             whole((components, atoms, channels)),
         ],
         out_specs=pl.BlockSpec((group * cap, 5 * channels), lambda i: (i, 0)),
         scratch_shapes=[pltpu.VMEM((atoms, components * channels), bf16)],
         compiler_params=pltpu.CompilerParams(dimension_semantics=("arbitrary",)),
+        cost_estimate=pl.CostEstimate(
+            flops=2 * owners * cap * atoms * components * channels,
+            bytes_accessed=8 * atoms * components * channels,
+            transcendentals=0,
+        ),
         name="owner",
     )(request, env)
+    if fields == 4:
+        lists = request[:, :, cap:].reshape(owners, -1)[:, :exports]
+    else:
+        lists = request[:, 4:, :].reshape(owners, -1)[:, :exports]
+    lists, sent = lax.optimization_barrier((lists, sent))
     received = lax.all_to_all(
         sent.reshape(owners, cap, 5 * channels),
         ("gy", "gz"),
@@ -289,62 +414,109 @@
     my_y, my_z = (lax.axis_index("gy"), lax.axis_index("gz"))
 
     def place(y, z):
-        dy, dz = (y ^ my_y, z ^ my_z)
-        flipped = jnp.zeros_like(dy)
-        for b in range(bits):
-            flipped = flipped | (((dy >> b) & 1) << (bits - 1 - b))
-        return (flipped * nz + dz) * block_rows
-
-    center_at = place(oy, oz) + pair_center
+        return ((y ^ my_y) * nz + (z ^ my_z)) * block_rows
+
     k = jnp.maximum(pair_neigh - atoms, 0)
     cell, member = (k // exports, k % exports)
     dx, dy, dz = (cell // 9 - 1, cell // 3 % 3 - 1, cell % 3 - 1)
     sy, sz = ((oy + dy) % ny, (oz + dz) % nz)
+    outside = atoms + member
     if nx > 2:
-        which = jnp.where(dx == 0, 0, jnp.where(dx < 0, 1, 2))
-    else:
-        which = jnp.where(dx == 0, 0, 1)
-    halo_at = place(sy, sz) + atoms + which * exports + member
-    neighbour_at = jnp.where(pair_neigh < atoms, place(oy, oz) + pair_neigh, halo_at)
-    pair_feat = jnp.concatenate([table[center_at], table[neighbour_at]], axis=1)
-    length = rows[7]
+        outside = outside + jnp.where(dx < 0, 0, exports)
+    home = place(oy, oz)
+    own = pair_neigh < atoms
+    listed = (pair_neigh >= atoms) & (dx == 0)
+    halo_at = place(sy, sz) + jnp.where(dx == 0, 0, outside)
+    entry = jnp.where(listed, (sy * nz + sz) * exports + member + 1, 0)
+    lists = jnp.concatenate([jnp.zeros((1,), f32), lists.reshape(-1)]).astype(jnp.int32)
+    neighbour_at = jnp.where(own, home + pair_neigh, halo_at)
+    index = jnp.stack([home + pair_center, neighbour_at, entry], axis=1).reshape(-1)
+    pieces[0, nz - 1], index, lists = lax.optimization_barrier((pieces[0, nz - 1], index, lists))
+    bit = ny // 2
+    while bit:
+        for (y, z), piece in list(pieces.items()):
+            pieces[y ^ bit, z] = swap(piece, "gy", bit)
+        bit //= 2
+    many = min(512, slots)
     basis = radial_proj.shape[0]
-    spacing = cutoff / (basis - 1)
-    centres = jnp.arange(basis).astype(f32) * spacing
-    radial = jnp.exp(-jnp.square((length[:, None] - centres[None, :]) / spacing))
-    both = jnp.concatenate([center_proj, neighbour_proj], axis=0)
-    before = jnp.dot(pair_feat, both, preferred_element_type=f32)
-    before = before + jnp.dot(radial, radial_proj.astype(f32), precision=lax.Precision.HIGHEST)
-    hidden = jax.nn.silu(before).astype(bf16)
-    latent = jax.nn.silu(jnp.dot(hidden, hidden_proj, preferred_element_type=f32)).astype(bf16)
-    mixed = jnp.dot(latent, split_proj, preferred_element_type=f32)
-
-    many = min(512, slots)
+    latent, mixed = pl.pallas_call(
+        functools.partial(latent_kernel, basis, block_rows),
+        grid=(slots // many,),
+        out_shape=(
+            jax.ShapeDtypeStruct((slots, latent_width), bf16),
+            jax.ShapeDtypeStruct((slots, 3 * channels), f32),
+        ),
+        in_specs=[
+            pl.BlockSpec(memory_space=pltpu.SMEM),
+            pl.BlockSpec(memory_space=pltpu.SMEM),
+            pl.BlockSpec((8, many), lambda i: (0, i)),
+        ]
+        + [pl.BlockSpec(memory_space=pltpu.VMEM)] * (owners + 4),
+        out_specs=(
+            pl.BlockSpec((many, latent_width), lambda i: (i, 0)),
+            pl.BlockSpec((many, 3 * channels), lambda i: (i, 0)),
+        ),
+        scratch_shapes=[
+            pltpu.VMEM((owners * block_rows, channels), f32),
+            pltpu.VMEM((2, many, channels), f32),
+        ],
+        compiler_params=pltpu.CompilerParams(dimension_semantics=("arbitrary",)),
+        cost_estimate=pl.CostEstimate(
+            flops=2 * slots * latent_width * (2 * latent_width + 3 * channels),
+            bytes_accessed=2 * owners * block_rows * channels,
+            transcendentals=4 * slots * latent_width,
+        ),
+        name="latent",
+    )(
+        index,
+        lists,
+        rows,
+        *[pieces[i // nz, i % nz] for i in range(owners)],
+        jnp.concatenate([center_proj, neighbour_proj], axis=0),
+        jnp.concatenate([radial_proj] * 3, axis=0),
+        hidden_proj,
+        split_proj,
+    )
+
     latent_out, vector_out, sums = pl.pallas_call(
-        functools.partial(final_kernel, owners),
-        grid=(slots // many,),
+        functools.partial(final_kernel, owners, cap, window),
+        grid=(slots // STEP,),
         out_shape=(
             jax.ShapeDtypeStruct((slots, latent_width), bf16),
             jax.ShapeDtypeStruct((3, slots, channels), bf16),
             jax.ShapeDtypeStruct((owners, atoms), f32),
         ),
         in_specs=[
-            pl.BlockSpec((8, many), lambda i: (0, i)),
+            pl.BlockSpec(memory_space=pltpu.SMEM),
+            pl.BlockSpec((8, STEP), lambda i: (0, i)),
             whole((owners * cap, 5 * channels)),
-            pl.BlockSpec((many, 3 * channels), lambda i: (i, 0)),
-            pl.BlockSpec((many, latent_width), lambda i: (i, 0)),
+            pl.BlockSpec((STEP, 3 * channels), lambda i: (i, 0)),
+            pl.BlockSpec((STEP, latent_width), lambda i: (i, 0)),
             whole(scalar_proj.shape),
             whole(path_gain.shape),
             whole((1, latent_width)),
         ],
         out_specs=(
-            pl.BlockSpec((many, latent_width), lambda i: (i, 0)),
-            pl.BlockSpec((3, many, channels), lambda i: (0, i, 0)),
+            pl.BlockSpec((STEP, latent_width), lambda i: (i, 0)),
+            pl.BlockSpec((3, STEP, channels), lambda i: (0, i, 0)),
             whole((owners, atoms)),
         ),
+        scratch_shapes=[
+            pltpu.VMEM((owners * window, 5 * channels), bf16),
+            pltpu.VMEM((STEP, 5 * channels), f32),
+        ],
         compiler_params=pltpu.CompilerParams(dimension_semantics=("arbitrary",)),
         name="final",
-    )(rows, received, mixed, latent, scalar_proj, path_gain, energy_proj.reshape(1, latent_width))
+    )(
+        starts,
+        rows,
+        received,
+        mixed,
+        latent,
+        scalar_proj,
+        path_gain,
+        energy_proj.reshape(1, latent_width),
+    )
     sums = lax.all_to_all(sums, ("gy", "gz"), split_axis=0, concat_axis=0, tiled=True)
     return (latent_out, vector_out, jnp.sum(sums, axis=0))
 
@@ -368,6 +540,7 @@
         P(),
         P(),
     )
+
     return jax.shard_map(
         local,
         mesh=mesh,

time: 224 us -> 232 us (1.036)
  waiting for transfers between devices: 83.1 us -> 125 us
  blocking collectives: 41.9 us -> 17.5 us
  local copies, waits for them, and re-layouts: 22.9 us -> 6.62 us
  Pallas kernels: 37.7 us -> 51.7 us
  starting transfers between devices: 14.2 us -> 24.1 us
  other arithmetic: 13.4 us -> 4.46 us
  matrix products: 8.29 us -> 0 us
    ppermute x5 -> x15, waiting for transfers between devices: 36.7 us -> 119 us  [swap(): lax.ppermute(x, axis, [(i, i ^ bit) for i in range(lax.axis_size(axis))])]
    all_to_all x1, waiting for transfers between devices: 45.1 us -> 0.01 us  [local(): lax.all_to_all(sent.reshape(owners, cap, 5 * channels), ('gy', 'gz'), spl...]
    all_to_all x1 -> x0, blocking collectives: 32.1 us -> none  [local(): lax.all_to_all(request, ('gy', 'gz'), split_axis=0, concat_axis=0, tiled=...]
    gather x2 -> x0, local copies, waits for them, and re-layouts: 18.4 us -> none  [local(): pair_feat = jnp.concatenate([table[center_at], table[neighbour_at]], axis=1)]
    pallas_call x2 -> x3, Pallas kernels: 24.1 us -> 38 us  [the longest x1 20.4 us: local(): pl.pallas_call(functools.partial(final_kernel, owners, cap, window), grid...]
    another operation x3 -> x1, other arithmetic: 11.9 us -> 0.02 us  [local(): jnp.stack([home + pair_center, neighbour_at, entry], axis=1).reshape(-1)]
    dot_general x4 -> x0, matrix products: 8.29 us -> none  [the longest x1 2.9 us: local(): mixed = jnp.dot(latent, split_proj, preferred_element_type=f32)]
    all_to_all x1, blocking collectives: 9.81 us -> 17.5 us  [local(): lax.all_to_all(sums, ('gy', 'gz'), split_axis=0, concat_axis=0, tiled=True)]
  transfers between devices with their start and end apart: 7 -> 18, of which waited for: 5 -> 6; matrix products, arithmetic and copies ran while one was open for 18% -> 2% of each run, Pallas kernels for 7% -> 7%
where the time goes in v2:
time: 232 us; the launch traced here: 231 us
  waiting for transfers between devices  125 us (54%)
  Pallas kernels  51.7 us (22%)
  starting transfers between devices  24.1 us (10%)
  blocking collectives  17.5 us (8%)
  local copies, waits for them, and re-layouts  6.62 us (3%)
  other arithmetic  4.46 us (2%)
    ppermute x15, waiting for transfers between devices, swap(): lax.ppermute(x, axis, [(i, i ^ bit) for i in range(lax.axis_size(axis))])  119 us
    pallas_call x1, Pallas kernels, local(): pl.pallas_call(functools.partial(final_kernel, owners, cap, window), grid...  20.4 us
    all_to_all x1, blocking collectives, local(): lax.all_to_all(sums, ('gy', 'gz'), split_axis=0, concat_axis=0, tiled=True)  17.5 us
    pallas_call x1, Pallas kernels, local(): pl.pallas_call(functools.partial(latent_kernel, basis, block_rows), grid=...  15.4 us
    pallas_call x1, Pallas kernels, local(): pl.pallas_call(functools.partial(owner_kernel, cap), grid=(owners // grou...  13.7 us
    ppermute x15, starting transfers between devices, swap(): lax.ppermute(x, axis, [(i, i ^ bit) for i in range(lax.axis_size(axis))])  10.4 us
    all_to_all x1, starting transfers between devices, local(): lax.all_to_all(request, ('gy', 'gz'), split_axis=0, concat_axis=0, tiled=...  5.94 us
    all_to_all x1, waiting for transfers between devices, local(): lax.all_to_all(request, ('gy', 'gz'), split_axis=0, concat_axis=0, tiled=...  5.63 us
  transfers between devices with their start and end apart: 18, of which 6 were waited for; matrix products, arithmetic and copies ran while one was open for 2% of the time, Pallas kernels for 7%

profile of v2, /device:TPU:0, one launch (start us, length us, event | category | flops | bytes accessed | tf_op | source)
XLA Modules:
  0.0 231.0 jit_solution(9060838615040531771)
XLA Ops:
  1.3 2.2 route.1
  3.4 0.7 compare_select_fusion
  4.1 1.7 gather_fusion
  5.8 3.0 %collective-permute-start = (bf16[256,128]{1,0:T(8,128)(2,1)S(1)}, bf16[256,128]{1,0:T(8,128)(2,1)S(1)}, u32[]{:S(2)}, u32[]{:S(2)}) collective-permute-start(bf16[256,128]{1,0:T(8,128)(2,1)S(1)} %gather_fusion), channel_id=1, source_target_pairs={{0,16},{16,0},{1,17},{17,1},{2,18},{18,2},{3,19},{19,3},{4,20},{20... | collective-permute-start | bytes 196616 | tf_op jit(solution)/shard_map/ppermute | solution.py:369
  8.9 5.9 %all-to-all-start = ((f32[16,4,256]{2,1,0:T(4,128)}), f32[16,4,256]{2,1,0:T(4,128)S(1)}, u32[]{:S(2)}, u32[]{:S(2)}) async-start(f32[16,4,256]{2,1,0:T(4,128)} %get-tuple-element.24), calls=%async_computation | async-start | bytes 131072 | tf_op jit(solution)/shard_map/all_to_all | solution.py:364
  14.8 0.0 collective-permute-done
  14.8 1.0 pad_maximum_fusion.refs_0_
  15.8 0.0 copy-start
  15.8 5.6 %all-to-all-done.request_ref = f32[16,4,256]{2,1,0:T(4,128)S(1)} async-done(((f32[16,4,256]{2,1,0:T(4,128)}), f32[16,4,256]{2,1,0:T(4,128)S(1)}, u32[]{:S(2)}, u32[]{:S(2)}) %all-to-all-start) | async-done | bytes 65568 | tf_op jit(solution)/shard_map/all_to_all | solution.py:364
  21.4 0.1 slice.3
  21.5 0.1 reshape.38
  21.6 0.5 copy-done.1
  22.1 13.7 %owner.1 = bf16[3072,640]{1,0:T(8,128)(2,1)} custom-call(f32[16,4,256]{2,1,0:T(4,128)} %copy-done.1, bf16[9,1024,128]{2,1,0:T(8,128)(2,1)} %bitcast.26), custom_call_target="tpu_custom_call" | custom-call | flops 7247757312 | bytes 9437184 | tf_op jit(solution)/shard_map/owner/pallas_call | solution.py:381
  35.8 4.7 %all-to-all-start.1 = ((bf16[16,192,640]{2,1,0:T(8,128)(2,1)}), bf16[16,192,640]{2,1,0:T(8,128)(2,1)}, u32[]{:S(2)}, u32[]{:S(2)}) async-start(bf16[16,192,640]{2,1,0:T(8,128)(2,1)} %bitcast.14), calls=%async_computation.1 | async-start | bytes 7864320 | tf_op jit(solution)/shard_map/all_to_all | solution.py:404
  40.5 0.0 copy-start.7
  40.5 0.0 copy-start.2
  40.5 0.0 copy-start.3
  40.5 0.1 add_select_fusion.11
  40.6 1.9 collective-permute-start.8
  42.5 0.0 collective-permute-start.4
  42.5 2.4 %collective-permute-start.3 = (bf16[1280,128]{1,0:T(8,128)(2,1)S(1)}, bf16[1280,128]{1,0:T(8,128)(2,1)S(1)}, u32[]{:S(2)}, u32[]{:S(2)}) collective-permute-start(bf16[1280,128]{1,0:T(8,128)(2,1)S(1)} %pad_maximum_fusion.refs_0_), channel_id=1, source_target_pairs={{0,2},{1,3},{2,0},{3,1},{4,6},{5,7},{6,4},{7,5},{8,10},{9,11},{10,... | collective-permute-start | bytes 983048 | tf_op jit(solution)/shard_map/ppermute | solution.py:312
  44.8 1.5 collective-permute-start.2
  46.3 0.5 collective-permute-start.1
  46.9 0.4 copy.20
  47.3 1.3 reshape.41.index_ref
  48.5 0.7 maximum_convert_fusion.lists_ref
  49.2 80.6 %collective-permute-done.1.refs_3_ = bf16[1280,128]{1,0:T(8,128)(2,1)S(1)} collective-permute-done((bf16[1280,128]{1,0:T(8,128)(2,1)S(1)}, bf16[1280,128]{1,0:T(8,128)(2,1)S(1)}, u32[]{:S(2)}, u32[]{:S(2)}) %collective-permute-start.1) | collective-permute-done | bytes 327712 | tf_op jit(solution)/shard_map/ppermute | solution.py:312
  129.9 0.0 collective-permute-done.8.refs_8_
  129.9 0.1 collective-permute-start.12
  129.9 20.3 %collective-permute-done.3.refs_2_ = bf16[1280,128]{1,0:T(8,128)(2,1)S(1)} collective-permute-done((bf16[1280,128]{1,0:T(8,128)(2,1)S(1)}, bf16[1280,128]{1,0:T(8,128)(2,1)S(1)}, u32[]{:S(2)}, u32[]{:S(2)}) %collective-permute-start.3) | collective-permute-done | bytes 327712 | tf_op jit(solution)/shard_map/ppermute | solution.py:312
  150.2 1.5 collective-permute-start.10
  151.8 0.0 collective-permute-start.6
  151.8 0.0 collective-permute-done.2.refs_1_
  151.8 0.6 collective-permute-start.9
  152.4 0.0 collective-permute-done.4.refs_4_
  152.4 1.5 collective-permute-start.11
  153.9 0.0 collective-permute-done.12.refs_12_
  153.9 0.0 collective-permute-start.7
  153.9 6.9 %collective-permute-done.10.refs_10_ = bf16[1280,128]{1,0:T(8,128)(2,1)S(1)} collective-permute-done((bf16[1280,128]{1,0:T(8,128)(2,1)S(1)}, bf16[1280,128]{1,0:T(8,128)(2,1)S(1)}, u32[]{:S(2)}, u32[]{:S(2)}) %collective-permute-start.10) | collective-permute-done | bytes 327712 | tf_op jit(solution)/shard_map/ppermute | solution.py:312
  160.8 0.0 collective-permute-start.5
  160.8 0.0 collective-permute-done.6.refs_6_
  160.8 0.5 collective-permute-start.14
  161.3 6.5 %collective-permute-done.9.refs_9_ = bf16[1280,128]{1,0:T(8,128)(2,1)S(1)} collective-permute-done((bf16[1280,128]{1,0:T(8,128)(2,1)S(1)}, bf16[1280,128]{1,0:T(8,128)(2,1)S(1)}, u32[]{:S(2)}, u32[]{:S(2)}) %collective-permute-start.9) | collective-permute-done | bytes 327712 | tf_op jit(solution)/shard_map/ppermute | solution.py:312
  167.9 0.0 collective-permute-start.13
  167.9 5.1 %collective-permute-done.11.refs_11_ = bf16[1280,128]{1,0:T(8,128)(2,1)S(1)} collective-permute-done((bf16[1280,128]{1,0:T(8,128)(2,1)S(1)}, bf16[1280,128]{1,0:T(8,128)(2,1)S(1)}, u32[]{:S(2)}, u32[]{:S(2)}) %collective-permute-start.11) | collective-permute-done | bytes 327712 | tf_op jit(solution)/shard_map/ppermute | solution.py:312
  172.9 0.0 collective-permute-start.15
  172.9 0.7 pad_maximum_fusion.2.refs_17_
  173.6 0.0 copy-done.3
  173.6 0.7 pad_maximum_fusion.1.refs_16_
  174.3 0.0 collective-permute-done.5.refs_5_
  174.3 0.0 collective-permute-done.7.refs_7_
  174.3 0.0 collective-permute-done.14.refs_14_
  174.4 0.0 collective-permute-done.13.refs_13_
  174.4 0.7 copy-done.19
  175.1 0.1 copy-done.18
  175.2 0.1 copy-done.20
  175.3 0.7 copy-done.21
  176.0 0.0 collective-permute-done.15.refs_15_
  176.1 15.4 %latent.1 = (bf16[2048,512]{1,0:T(8,128)(2,1)}, f32[2048,384]{1,0:T(8,128)}) custom-call(s32[6144]{0:T(1024)} %reshape.41.index_ref, s32[4097]{0:T(1024)} %maximum_convert_fusion.lists_ref, f32[8,2048]{1,0:T(8,128)} %get-tuple-element.22.rows_ref, bf16[1280,128]{1,0:T(8,128)(2,1)} %copy-done, bf16[1280,128]{1,0:T(8,128)(2,1)} %copy-done.11, ...), custom_call_target="tpu_custom_call" | custom-call | flops 2952790016 | bytes 5242880 | tf_op jit(solution)/shard_map/latent/pallas_call | solution.py:442
  191.6 0.0 all-to-all-done.1
  191.6 20.4 %final.1 = (bf16[2048,512]{1,0:T(8,128)(2,1)}, bf16[3,2048,128]{2,1,0:T(8,128)(2,1)}, f32[16,1024]{1,0:T(8,128)}) custom-call(s32[16,128]{1,0:T(8,128)} %get-tuple-element.20.starts_ref, f32[8,2048]{1,0:T(8,128)} %get-tuple-element.22.rows_ref, bf16[3072,640]{1,0:T(8,128)(2,1)} %bitcast.5.env_ref, f32[2048,384]{1,0:T(8,128)} %get-tuple-element.32.mixed_ref, ...), custom_call_target="tpu_custom_call" | custom-call | tf_op jit(solution)/shard_map/final/pallas_call | solution.py:481
  212.0 0.9 copy.21
  212.9 17.5 %all_to_all.19 = f32[16,1,1024]{2,1,0:T(1,128)S(1)} all-to-all(f32[16,1,1024]{2,1,0:T(1,128)S(1)} %copy.21), channel_id=1, replica_groups=mesh['gx'=2,'gy'=4,'gz'=4] {'gy','gz'}, dimensions={0} | all-to-all | bytes 131072 | tf_op jit(solution)/shard_map/all_to_all | solution.py:520
  230.4 0.6 reduce_sum.9
  (37 shorter events, 0.1 us)
Async XLA Ops:
  5.8 9.0 %collective-permute-start = (bf16[256,128]{1,0:T(8,128)(2,1)S(1)}, bf16[256,128]{1,0:T(8,128)(2,1)S(1)}, u32[]{:S(2)}, u32[]{:S(2)}) collective-permute-start(bf16[256,128]{1,0:T(8,128)(2,1)S(1)} %gather_fusion), channel_id=1, source_target_pairs={{0,16},{16,0},{1,17},{17,1},{2,18},{18,2},{3,19},{19,3},{4,20},{20... | collective-permute-start | bytes 196616 | tf_op jit(solution)/shard_map/ppermute | solution.py:369
  8.9 12.6 %all-to-all-start = ((f32[16,4,256]{2,1,0:T(4,128)}), f32[16,4,256]{2,1,0:T(4,128)S(1)}, u32[]{:S(2)}, u32[]{:S(2)}) async-start(f32[16,4,256]{2,1,0:T(4,128)} %get-tuple-element.24), calls=%async_computation | async-start | bytes 131072 | tf_op jit(solution)/shard_map/all_to_all | solution.py:364
  15.8 30.5 %copy-start = (bf16[1280,128]{1,0:T(8,128)(2,1)}, bf16[1280,128]{1,0:T(8,128)(2,1)S(1)}, u32[]{:S(2)}) copy-start(bf16[1280,128]{1,0:T(8,128)(2,1)S(1)} %pad_maximum_fusion.refs_0_) | copy-start | bytes 983044
  21.4 0.6 copy-start.1
  35.8 4.7 %copy-start.4 = (s32[2048,1]{0,1:T(1,128)S(1)}, s32[2048,1]{0,1:T(1,128)}, u32[]{:S(2)}) copy-start(s32[2048,1]{0,1:T(1,128)} %param.21) | copy-start | bytes 24580
  35.8 4.7 %copy-start.5 = (s32[2048]{0:T(1024)S(1)}, s32[2048]{0:T(1024)}, u32[]{:S(2)}) copy-start(s32[2048]{0:T(1024)} %param.20) | copy-start | bytes 24580
  35.8 4.8 %copy-start.6 = (s32[2048]{0:T(1024)S(1)}, s32[2048]{0:T(1024)}, u32[]{:S(2)}) copy-start(s32[2048]{0:T(1024)} %param.22) | copy-start | bytes 24580
  35.8 155.8 %all-to-all-start.1 = ((bf16[16,192,640]{2,1,0:T(8,128)(2,1)}), bf16[16,192,640]{2,1,0:T(8,128)(2,1)}, u32[]{:S(2)}, u32[]{:S(2)}) async-start(bf16[16,192,640]{2,1,0:T(8,128)(2,1)} %bitcast.14), calls=%async_computation.1 | async-start | bytes 7864320 | tf_op jit(solution)/shard_map/all_to_all | solution.py:404
  40.5 132.5 %copy-start.7 = (bf16[8,512]{1,0:T(8,128)(2,1)S(1)}, bf16[8,512]{1,0:T(8,128)(2,1)}, u32[]{:S(2)}) copy-start(bf16[8,512]{1,0:T(8,128)(2,1)} %param.26) | copy-start | bytes 24580
  40.5 133.1 %copy-start.2 = (bf16[128,512]{1,0:T(8,128)(2,1)S(1)}, bf16[128,512]{1,0:T(8,128)(2,1)}, u32[]{:S(2)}) copy-start(bf16[128,512]{1,0:T(8,128)(2,1)} %param.25) | copy-start | bytes 393220
  40.5 133.1 %copy-start.3 = (bf16[128,512]{1,0:T(8,128)(2,1)S(1)}, bf16[128,512]{1,0:T(8,128)(2,1)}, u32[]{:S(2)}) copy-start(bf16[128,512]{1,0:T(8,128)(2,1)} %param.24) | copy-start | bytes 393220
  40.6 89.3 %collective-permute-start.8 = (bf16[1280,128]{1,0:T(8,128)(2,1)S(1)}, bf16[1280,128]{1,0:T(8,128)(2,1)S(1)}, u32[]{:S(2)}, u32[]{:S(2)}) collective-permute-start(bf16[1280,128]{1,0:T(8,128)(2,1)S(1)} %pad_maximum_fusion.refs_0_), channel_id=1, source_target_pairs={{0,8},{4,12},{8,0},{12,4},{1,9},{5,13},{9,1},{13,5},{2,10},{6,14},... | collective-permute-start | bytes 983048 | tf_op jit(solution)/shard_map/ppermute | solution.py:312
  42.5 109.9 %collective-permute-start.4 = (bf16[1280,128]{1,0:T(8,128)(2,1)S(1)}, bf16[1280,128]{1,0:T(8,128)(2,1)S(1)}, u32[]{:S(2)}, u32[]{:S(2)}) collective-permute-start(bf16[1280,128]{1,0:T(8,128)(2,1)S(1)} %pad_maximum_fusion.refs_0_), channel_id=1, source_target_pairs={{0,4},{4,0},{8,12},{12,8},{1,5},{5,1},{9,13},{13,9},{2,6},{6,2},{1... | collective-permute-start | bytes 983048 | tf_op jit(solution)/shard_map/ppermute | solution.py:312
  42.5 107.8 %collective-permute-start.3 = (bf16[1280,128]{1,0:T(8,128)(2,1)S(1)}, bf16[1280,128]{1,0:T(8,128)(2,1)S(1)}, u32[]{:S(2)}, u32[]{:S(2)}) collective-permute-start(bf16[1280,128]{1,0:T(8,128)(2,1)S(1)} %pad_maximum_fusion.refs_0_), channel_id=1, source_target_pairs={{0,2},{1,3},{2,0},{3,1},{4,6},{5,7},{6,4},{7,5},{8,10},{9,11},{10,... | collective-permute-start | bytes 983048 | tf_op jit(solution)/shard_map/ppermute | solution.py:312
  44.8 106.9 %collective-permute-start.2 = (bf16[1280,128]{1,0:T(8,128)(2,1)S(1)}, bf16[1280,128]{1,0:T(8,128)(2,1)S(1)}, u32[]{:S(2)}, u32[]{:S(2)}) collective-permute-start(bf16[1280,128]{1,0:T(8,128)(2,1)S(1)} %pad_maximum_fusion.refs_0_), channel_id=1, source_target_pairs={{0,1},{1,0},{2,3},{3,2},{4,5},{5,4},{6,7},{7,6},{8,9},{9,8},{10,11... | collective-permute-start | bytes 983048 | tf_op jit(solution)/shard_map/ppermute | solution.py:312
  46.3 83.5 %collective-permute-start.1 = (bf16[1280,128]{1,0:T(8,128)(2,1)S(1)}, bf16[1280,128]{1,0:T(8,128)(2,1)S(1)}, u32[]{:S(2)}, u32[]{:S(2)}) collective-permute-start(bf16[1280,128]{1,0:T(8,128)(2,1)S(1)} %pad_maximum_fusion.refs_0_), channel_id=1, source_target_pairs={{0,3},{1,2},{2,1},{3,0},{4,7},{5,6},{6,5},{7,4},{8,11},{9,10},{10,... | collective-permute-start | bytes 983048 | tf_op jit(solution)/shard_map/ppermute | solution.py:312
  129.9 46.2 %copy-start.12 = (bf16[1280,128]{1,0:T(8,128)(2,1)}, bf16[1280,128]{1,0:T(8,128)(2,1)S(1)}, u32[]{:S(2)}) copy-start(bf16[1280,128]{1,0:T(8,128)(2,1)S(1)} %collective-permute-done.1.refs_3_) | copy-start | bytes 983044
  129.9 46.2 %copy-start.8 = (bf16[1280,128]{1,0:T(8,128)(2,1)}, bf16[1280,128]{1,0:T(8,128)(2,1)S(1)}, u32[]{:S(2)}) copy-start(bf16[1280,128]{1,0:T(8,128)(2,1)S(1)} %collective-permute-done.8.refs_8_) | copy-start | bytes 983044
  129.9 24.0 %collective-permute-start.12 = (bf16[1280,128]{1,0:T(8,128)(2,1)S(1)}, bf16[1280,128]{1,0:T(8,128)(2,1)S(1)}, u32[]{:S(2)}, u32[]{:S(2)}) collective-permute-start(bf16[1280,128]{1,0:T(8,128)(2,1)S(1)} %collective-permute-done.8.refs_8_), channel_id=1, source_target_pairs={{0,4},{4,0},{8,12},{12,8},{1,5},{5,1},{9,13},{13,9},{2,6},{6,2},{1... | collective-permute-start | bytes 983048 | tf_op jit(solution)/shard_map/ppermute | solution.py:312
  150.2 25.8 %copy-start.10 = (bf16[1280,128]{1,0:T(8,128)(2,1)}, bf16[1280,128]{1,0:T(8,128)(2,1)S(1)}, u32[]{:S(2)}) copy-start(bf16[1280,128]{1,0:T(8,128)(2,1)S(1)} %collective-permute-done.3.refs_2_) | copy-start | bytes 983044
  150.2 10.6 %collective-permute-start.10 = (bf16[1280,128]{1,0:T(8,128)(2,1)S(1)}, bf16[1280,128]{1,0:T(8,128)(2,1)S(1)}, u32[]{:S(2)}, u32[]{:S(2)}) collective-permute-start(bf16[1280,128]{1,0:T(8,128)(2,1)S(1)} %collective-permute-done.3.refs_2_), channel_id=1, source_target_pairs={{0,8},{4,12},{8,0},{12,4},{1,9},{5,13},{9,1},{13,5},{2,10},{6,14},... | collective-permute-start | bytes 983048 | tf_op jit(solution)/shard_map/ppermute | solution.py:312
  151.8 9.1 %collective-permute-start.6 = (bf16[1280,128]{1,0:T(8,128)(2,1)S(1)}, bf16[1280,128]{1,0:T(8,128)(2,1)S(1)}, u32[]{:S(2)}, u32[]{:S(2)}) collective-permute-start(bf16[1280,128]{1,0:T(8,128)(2,1)S(1)} %collective-permute-done.3.refs_2_), channel_id=1, source_target_pairs={{0,4},{4,0},{8,12},{12,8},{1,5},{5,1},{9,13},{13,9},{2,6},{6,2},{1... | collective-permute-start | bytes 983048 | tf_op jit(solution)/shard_map/ppermute | solution.py:312
  151.8 24.3 %copy-start.11 = (bf16[1280,128]{1,0:T(8,128)(2,1)}, bf16[1280,128]{1,0:T(8,128)(2,1)S(1)}, u32[]{:S(2)}) copy-start(bf16[1280,128]{1,0:T(8,128)(2,1)S(1)} %collective-permute-done.2.refs_1_) | copy-start | bytes 983044
  151.8 16.1 %collective-permute-start.9 = (bf16[1280,128]{1,0:T(8,128)(2,1)S(1)}, bf16[1280,128]{1,0:T(8,128)(2,1)S(1)}, u32[]{:S(2)}, u32[]{:S(2)}) collective-permute-start(bf16[1280,128]{1,0:T(8,128)(2,1)S(1)} %collective-permute-done.2.refs_1_), channel_id=1, source_target_pairs={{0,8},{4,12},{8,0},{12,4},{1,9},{5,13},{9,1},{13,5},{2,10},{6,14},... | collective-permute-start | bytes 983048 | tf_op jit(solution)/shard_map/ppermute | solution.py:312
  152.4 23.7 %copy-start.9 = (bf16[1280,128]{1,0:T(8,128)(2,1)}, bf16[1280,128]{1,0:T(8,128)(2,1)S(1)}, u32[]{:S(2)}) copy-start(bf16[1280,128]{1,0:T(8,128)(2,1)S(1)} %collective-permute-done.4.refs_4_) | copy-start | bytes 983044
  152.4 20.6 %collective-permute-start.11 = (bf16[1280,128]{1,0:T(8,128)(2,1)S(1)}, bf16[1280,128]{1,0:T(8,128)(2,1)S(1)}, u32[]{:S(2)}, u32[]{:S(2)}) collective-permute-start(bf16[1280,128]{1,0:T(8,128)(2,1)S(1)} %collective-permute-done.1.refs_3_), channel_id=1, source_target_pairs={{0,8},{4,12},{8,0},{12,4},{1,9},{5,13},{9,1},{13,5},{2,10},{6,14},... | collective-permute-start | bytes 983048 | tf_op jit(solution)/shard_map/ppermute | solution.py:312
  153.9 22.2 %copy-start.13 = (bf16[1280,128]{1,0:T(8,128)(2,1)}, bf16[1280,128]{1,0:T(8,128)(2,1)S(1)}, u32[]{:S(2)}) copy-start(bf16[1280,128]{1,0:T(8,128)(2,1)S(1)} %collective-permute-done.12.refs_12_) | copy-start | bytes 983044
  153.9 20.4 %collective-permute-start.7 = (bf16[1280,128]{1,0:T(8,128)(2,1)S(1)}, bf16[1280,128]{1,0:T(8,128)(2,1)S(1)}, u32[]{:S(2)}, u32[]{:S(2)}) collective-permute-start(bf16[1280,128]{1,0:T(8,128)(2,1)S(1)} %collective-permute-done.1.refs_3_), channel_id=1, source_target_pairs={{0,4},{4,0},{8,12},{12,8},{1,5},{5,1},{9,13},{13,9},{2,6},{6,2},{1... | collective-permute-start | bytes 983048 | tf_op jit(solution)/shard_map/ppermute | solution.py:312
  160.8 15.3 %copy-start.14 = (bf16[1280,128]{1,0:T(8,128)(2,1)}, bf16[1280,128]{1,0:T(8,128)(2,1)S(1)}, u32[]{:S(2)}) copy-start(bf16[1280,128]{1,0:T(8,128)(2,1)S(1)} %collective-permute-done.10.refs_10_) | copy-start | bytes 983044
  160.8 13.5 %collective-permute-start.5 = (bf16[1280,128]{1,0:T(8,128)(2,1)S(1)}, bf16[1280,128]{1,0:T(8,128)(2,1)S(1)}, u32[]{:S(2)}, u32[]{:S(2)}) collective-permute-start(bf16[1280,128]{1,0:T(8,128)(2,1)S(1)} %collective-permute-done.2.refs_1_), channel_id=1, source_target_pairs={{0,4},{4,0},{8,12},{12,8},{1,5},{5,1},{9,13},{13,9},{2,6},{6,2},{1... | collective-permute-start | bytes 983048 | tf_op jit(solution)/shard_map/ppermute | solution.py:312
  160.8 15.3 %copy-start.15 = (bf16[1280,128]{1,0:T(8,128)(2,1)}, bf16[1280,128]{1,0:T(8,128)(2,1)S(1)}, u32[]{:S(2)}) copy-start(bf16[1280,128]{1,0:T(8,128)(2,1)S(1)} %collective-permute-done.6.refs_6_) | copy-start | bytes 983044
  160.8 13.5 %collective-permute-start.14 = (bf16[1280,128]{1,0:T(8,128)(2,1)S(1)}, bf16[1280,128]{1,0:T(8,128)(2,1)S(1)}, u32[]{:S(2)}, u32[]{:S(2)}) collective-permute-start(bf16[1280,128]{1,0:T(8,128)(2,1)S(1)} %collective-permute-done.10.refs_10_), channel_id=1, source_target_pairs={{0,4},{4,0},{8,12},{12,8},{1,5},{5,1},{9,13},{13,9},{2,6},{6,2},{1... | collective-permute-start | bytes 983048 | tf_op jit(solution)/shard_map/ppermute | solution.py:312
  167.9 6.5 %copy-start.16 = (bf16[1280,128]{1,0:T(8,128)(2,1)}, bf16[1280,128]{1,0:T(8,128)(2,1)S(1)}, u32[]{:S(2)}) copy-start(bf16[1280,128]{1,0:T(8,128)(2,1)S(1)} %collective-permute-done.9.refs_9_) | copy-start | bytes 983044
  167.9 6.5 %collective-permute-start.13 = (bf16[1280,128]{1,0:T(8,128)(2,1)S(1)}, bf16[1280,128]{1,0:T(8,128)(2,1)S(1)}, u32[]{:S(2)}, u32[]{:S(2)}) collective-permute-start(bf16[1280,128]{1,0:T(8,128)(2,1)S(1)} %collective-permute-done.9.refs_9_), channel_id=1, source_target_pairs={{0,4},{4,0},{8,12},{12,8},{1,5},{5,1},{9,13},{13,9},{2,6},{6,2},{1... | collective-permute-start | bytes 983048 | tf_op jit(solution)/shard_map/ppermute | solution.py:312
  172.9 3.2 %copy-start.17 = (bf16[1280,128]{1,0:T(8,128)(2,1)}, bf16[1280,128]{1,0:T(8,128)(2,1)S(1)}, u32[]{:S(2)}) copy-start(bf16[1280,128]{1,0:T(8,128)(2,1)S(1)} %collective-permute-done.11.refs_11_) | copy-start | bytes 983044
  172.9 3.1 %collective-permute-start.15 = (bf16[1280,128]{1,0:T(8,128)(2,1)S(1)}, bf16[1280,128]{1,0:T(8,128)(2,1)}, u32[]{:S(2)}, u32[]{:S(2)}) collective-permute-start(bf16[1280,128]{1,0:T(8,128)(2,1)S(1)} %collective-permute-done.11.refs_11_), channel_id=1, source_target_pairs={{0,4},{4,0},{8,12},{12,8},{1,5},{5,1},{9,13},{13,9},{2,6},{6,2},{1... | collective-permute-start | bytes 983048 | tf_op jit(solution)/shard_map/ppermute | solution.py:312
  174.3 0.7 copy-start.19
  174.3 0.8 copy-start.18
  174.4 0.9 copy-start.20
  175.3 0.7 copy-start.21

commit v3 on v2

--- a/solution.py
+++ b/solution.py
@@ -18,6 +18,11 @@
 LANES = 128
 STEP = 256
 NT = (((1,), (1,)), ((), ()))
+
+
+def silu(v):
+    half = 0.5 * v
+    return half + half * jnp.tanh(half)
 
 
 def split3(v):
@@ -154,7 +159,7 @@
     out_ref[:, keep:] = total.astype(bf16)
 
 
-def latent_kernel(basis, block_rows, index_ref, lists_ref, rows_ref, *refs):
+def latent_kernel(basis, index_ref, lists_ref, rows_ref, *refs):
     pieces = refs[:-8]
     both_ref, radial_ref, hidden_ref, split_ref, latent_ref, mixed_ref = refs[-8:-2]
     table_ref, feat_ref = refs[-2:]
@@ -162,8 +167,10 @@
 
     @pl.when(pl.program_id(0) == 0)
     def _():
-        for i, piece in enumerate(pieces):
-            table_ref[i * block_rows : (i + 1) * block_rows, :] = piece[...].astype(f32)
+        at = 0
+        for piece in pieces:
+            table_ref[at : at + piece.shape[0], :] = piece[...].astype(f32)
+            at += piece.shape[0]
 
     start = pl.program_id(0) * many
     unroll = 16
@@ -189,9 +196,9 @@
     feat = jnp.concatenate([feat_ref[0], feat_ref[1]], axis=1).astype(bf16)
     before = jnp.dot(feat, both_ref[...], preferred_element_type=f32)
     before = before + jnp.dot(radial, radial_ref[...], preferred_element_type=f32)
-    hidden = (before * jax.nn.sigmoid(before)).astype(bf16)
+    hidden = silu(before).astype(bf16)
     after = jnp.dot(hidden, hidden_ref[...], preferred_element_type=f32)
-    latent = (after * jax.nn.sigmoid(after)).astype(bf16)
+    latent = silu(after).astype(bf16)
     latent_ref[...] = latent
     mixed_ref[...] = jnp.dot(latent, split_ref[...], preferred_element_type=f32)
 
@@ -213,39 +220,46 @@
     sums_ref,
     near_ref,
     found_ref,
+    total_ref,
 ):
     many = rows_ref.shape[1]
     places = env_ref.shape[0]
     channels = gain_ref.shape[1]
     atoms = sums_ref.shape[1]
     columns = jnp.transpose(rows_ref[...])
-    step = pl.program_id(0)
-
-    def pick(column, size):
-        hit = columns[:, column : column + 1].astype(jnp.int32) == lax.broadcasted_iota(
-            jnp.int32, (many, size), 1
-        )
+
+    def pick(part, column, size):
+        wanted = columns[part * STEP : (part + 1) * STEP, column : column + 1]
+        hit = wanted.astype(jnp.int32) == lax.broadcasted_iota(jnp.int32, (STEP, size), 1)
         return jnp.where(hit, 1.0, 0.0).astype(bf16)
 
-    fits = True
-    bases = []
-    for o in range(owners):
-        base = jnp.minimum(starts_ref[o, step] // 16 * 16, cap - window)
-        bases.append(base)
-        fits = fits & (starts_ref[o, step + 1] <= base + window)
-
-    @pl.when(fits)
-    def _():
+    def find(part):
+        step = pl.program_id(0) * (many // STEP) + part
+        here = pl.ds(part * STEP, STEP)
+        fits = True
+        bases = []
         for o in range(owners):
-            at = pl.multiple_of(o * cap + bases[o], 16)
-            near_ref[o * window : (o + 1) * window, :] = env_ref[pl.ds(at, window), :]
-        found_ref[...] = jnp.dot(
-            pick(3, owners * window), near_ref[...], preferred_element_type=f32
-        )
-
-    @pl.when(jnp.logical_not(fits))
-    def _():
-        found_ref[...] = jnp.dot(pick(4, places), env_ref[...], preferred_element_type=f32)
+            base = jnp.minimum(starts_ref[o, step] // 16 * 16, cap - window)
+            bases.append(base)
+            fits = fits & (starts_ref[o, step + 1] <= base + window)
+
+        @pl.when(fits)
+        def _():
+            for o in range(owners):
+                at = pl.multiple_of(o * cap + bases[o], 16)
+                near_ref[o * window : (o + 1) * window, :] = env_ref[pl.ds(at, window), :]
+            found_ref[here, :] = jnp.dot(
+                pick(part, 3, owners * window), near_ref[...], preferred_element_type=f32
+            )
+
+        @pl.when(jnp.logical_not(fits))
+        def _():
+            found_ref[here, :] = jnp.dot(
+                pick(part, 4, places), env_ref[...], preferred_element_type=f32
+            )
+
+    for part in range(many // STEP):
+        find(part)
 
     env = found_ref[...]
     part = lambda i: env[:, i * channels : (i + 1) * channels]
@@ -279,7 +293,7 @@
         )
         vector_out_ref[m] = jnp.where(live, value, 0.0).astype(bf16)
     update = jnp.dot(invariants, scalar_ref[...], preferred_element_type=f32)
-    update = update * jax.nn.sigmoid(update)
+    update = silu(update)
     latent = jnp.where(live, latent_ref[...].astype(f32) + update, 0.0).astype(bf16)
     latent_out_ref[...] = latent
     energy = jnp.sum(latent.astype(f32) * energy_ref[...], axis=1, keepdims=True)
@@ -288,20 +302,23 @@
     spread = jnp.zeros((many, LANES), f32)
     for i, piece in enumerate(split3(energy)):
         spread = spread + jnp.where(lane == owner + i * owners, piece, 0.0)
-    spread = jnp.transpose(spread).astype(bf16)
-    center = columns[:, 6:7].astype(jnp.int32)
-    of_atom = center == lax.broadcasted_iota(jnp.int32, (many, atoms), 1)
+    center = rows_ref[6:7, :].astype(jnp.int32)
+    of_atom = center == lax.broadcasted_iota(jnp.int32, (atoms, many), 0)
     of_atom = jnp.where(of_atom, 1.0, 0.0).astype(bf16)
-    sums = jnp.dot(spread, of_atom, preferred_element_type=f32)
-    sums = sums[:owners] + sums[owners : 2 * owners] + sums[2 * owners : 3 * owners]
+    sums = jnp.dot(of_atom, spread.astype(bf16), preferred_element_type=f32)
 
     @pl.when(pl.program_id(0) == 0)
     def _():
-        sums_ref[...] = sums
+        total_ref[...] = sums
 
     @pl.when(pl.program_id(0) > 0)
     def _():
-        sums_ref[...] = sums_ref[...] + sums
+        total_ref[...] = total_ref[...] + sums
+
+    @pl.when(pl.program_id(0) == pl.num_programs(0) - 1)
+    def _():
+        total = jnp.transpose(total_ref[...])
+        sums_ref[...] = sum(total[i * owners : (i + 1) * owners] for i in range(3))
 
 
 def whole(shape):
@@ -310,6 +327,14 @@
 
 def swap(x, axis, bit):
     return lax.ppermute(x, axis, [(i, i ^ bit) for i in range(lax.axis_size(axis))])
+
+
+def across(pieces, size):
+    bit = size // 2
+    while bit:
+        for (y, z), piece in list(pieces.items()):
+            pieces[y ^ bit, z] = swap(piece, "gy", bit)
+        bit //= 2
 
 
 def local(
@@ -360,21 +385,14 @@
         pair_vec,
         export_index.reshape(1, exports),
     )
-    export_index, rows = lax.optimization_barrier((export_index, rows))
     request = lax.all_to_all(request, ("gy", "gz"), split_axis=0, concat_axis=0, tiled=True)
 
-    exported = atom_feat[export_index]
-    up = [(i, (i + 1) % nx) for i in range(nx)]
-    down = [(j, i) for i, j in up]
-    parts = [atom_feat, lax.ppermute(exported, "gx", up)]
-    if nx > 2:
-        parts.append(lax.ppermute(exported, "gx", down))
-    block = jnp.concatenate(parts, axis=0)
-    block_rows = block.shape[0]
-    block, request = lax.optimization_barrier((block, request))
-    pieces = {(0, 0): block}
+    my_y, my_z = (lax.axis_index("gy"), lax.axis_index("gz"))
+    feat, request = lax.optimization_barrier((atom_feat, request))
+    feats = {(0, 0): feat}
     for k in range(1, nz):
-        pieces[0, k] = swap(block, "gz", k)
+        feats[0, k] = swap(feat, "gz", k)
+    across(feats, ny)
 
     group = min(4, owners)
     env = jnp.transpose(atom_env, (1, 0, 2))
@@ -409,38 +427,50 @@
         tiled=True,
     ).reshape(owners * cap, 5 * channels)
 
+    lists = lists.astype(jnp.int32)
+    along = lax.dynamic_index_in_dim(lists.reshape(ny, nz, exports), my_y, 0, keepdims=False)
+    along = along[jnp.arange(nz) ^ my_z] + jnp.arange(nz)[:, None] * atoms
+    column = jnp.concatenate([feats[0, k] for k in range(nz)], axis=0)
+    exported = column[along.reshape(-1)]
+    up = [(i, (i + 1) % nx) for i in range(nx)]
+    down = [(j, i) for i, j in up]
+    beyond = [lax.ppermute(exported, "gx", up)]
+    if nx > 2:
+        beyond.append(lax.ppermute(exported, "gx", down))
+    beyond = jnp.concatenate(beyond, axis=0)
+
     owner = pair_owner[:, 0]
     oy, oz = (owner // nz, owner % nz)
-    my_y, my_z = (lax.axis_index("gy"), lax.axis_index("gz"))
-
-    def place(y, z):
-        return ((y ^ my_y) * nz + (z ^ my_z)) * block_rows
+
+    def cell_of(y, z):
+        return (y ^ my_y) * nz + (z ^ my_z)
 
     k = jnp.maximum(pair_neigh - atoms, 0)
     cell, member = (k // exports, k % exports)
     dx, dy, dz = (cell // 9 - 1, cell // 3 % 3 - 1, cell % 3 - 1)
     sy, sz = ((oy + dy) % ny, (oz + dz) % nz)
-    outside = atoms + member
+    sides = beyond.shape[0] // (nz * exports)
+    outside = (sy ^ my_y) * sides
     if nx > 2:
-        outside = outside + jnp.where(dx < 0, 0, exports)
-    home = place(oy, oz)
+        outside = outside + jnp.where(dx < 0, 0, 1)
+    outside = owners * atoms + (outside * nz + (sz ^ my_z)) * exports + member
+    home = cell_of(oy, oz) * atoms
     own = pair_neigh < atoms
     listed = (pair_neigh >= atoms) & (dx == 0)
-    halo_at = place(sy, sz) + jnp.where(dx == 0, 0, outside)
+    halo_at = jnp.where(dx == 0, cell_of(sy, sz) * atoms, outside)
     entry = jnp.where(listed, (sy * nz + sz) * exports + member + 1, 0)
-    lists = jnp.concatenate([jnp.zeros((1,), f32), lists.reshape(-1)]).astype(jnp.int32)
+    lists = jnp.concatenate([jnp.zeros((1,), jnp.int32), lists.reshape(-1)])
     neighbour_at = jnp.where(own, home + pair_neigh, halo_at)
     index = jnp.stack([home + pair_center, neighbour_at, entry], axis=1).reshape(-1)
-    pieces[0, nz - 1], index, lists = lax.optimization_barrier((pieces[0, nz - 1], index, lists))
-    bit = ny // 2
-    while bit:
-        for (y, z), piece in list(pieces.items()):
-            pieces[y ^ bit, z] = swap(piece, "gy", bit)
-        bit //= 2
+    beyond, index, lists = lax.optimization_barrier((beyond, index, lists))
+    edges = {(0, 0): beyond}
+    across(edges, ny)
+    pieces = [feats[i // nz, i % nz] for i in range(owners)] + [edges[i, 0] for i in range(ny)]
+    table_rows = sum(piece.shape[0] for piece in pieces)
     many = min(512, slots)
     basis = radial_proj.shape[0]
     latent, mixed = pl.pallas_call(
-        functools.partial(latent_kernel, basis, block_rows),
+        functools.partial(latent_kernel, basis),
         grid=(slots // many,),
         out_shape=(
             jax.ShapeDtypeStruct((slots, latent_width), bf16),
@@ -451,19 +481,19 @@
             pl.BlockSpec(memory_space=pltpu.SMEM),
             pl.BlockSpec((8, many), lambda i: (0, i)),
         ]
-        + [pl.BlockSpec(memory_space=pltpu.VMEM)] * (owners + 4),
+        + [pl.BlockSpec(memory_space=pltpu.VMEM)] * (len(pieces) + 4),
         out_specs=(
             pl.BlockSpec((many, latent_width), lambda i: (i, 0)),
             pl.BlockSpec((many, 3 * channels), lambda i: (i, 0)),
         ),
         scratch_shapes=[
-            pltpu.VMEM((owners * block_rows, channels), f32),
+            pltpu.VMEM((table_rows, channels), f32),
             pltpu.VMEM((2, many, channels), f32),
         ],
         compiler_params=pltpu.CompilerParams(dimension_semantics=("arbitrary",)),
         cost_estimate=pl.CostEstimate(
             flops=2 * slots * latent_width * (2 * latent_width + 3 * channels),
-            bytes_accessed=2 * owners * block_rows * channels,
+            bytes_accessed=2 * table_rows * channels,
             transcendentals=4 * slots * latent_width,
         ),
         name="latent",
@@ -471,7 +501,7 @@
         index,
         lists,
         rows,
-        *[pieces[i // nz, i % nz] for i in range(owners)],
+        *pieces,
         jnp.concatenate([center_proj, neighbour_proj], axis=0),
         jnp.concatenate([radial_proj] * 3, axis=0),
         hidden_proj,
@@ -480,7 +510,7 @@
 
     latent_out, vector_out, sums = pl.pallas_call(
         functools.partial(final_kernel, owners, cap, window),
-        grid=(slots // STEP,),
+        grid=(slots // many,),
         out_shape=(
             jax.ShapeDtypeStruct((slots, latent_width), bf16),
             jax.ShapeDtypeStruct((3, slots, channels), bf16),
@@ -488,22 +518,23 @@
         ),
         in_specs=[
             pl.BlockSpec(memory_space=pltpu.SMEM),
-            pl.BlockSpec((8, STEP), lambda i: (0, i)),
+            pl.BlockSpec((8, many), lambda i: (0, i)),
             whole((owners * cap, 5 * channels)),
-            pl.BlockSpec((STEP, 3 * channels), lambda i: (i, 0)),
-            pl.BlockSpec((STEP, latent_width), lambda i: (i, 0)),
+            pl.BlockSpec((many, 3 * channels), lambda i: (i, 0)),
+            pl.BlockSpec((many, latent_width), lambda i: (i, 0)),
             whole(scalar_proj.shape),
             whole(path_gain.shape),
             whole((1, latent_width)),
         ],
         out_specs=(
-            pl.BlockSpec((STEP, latent_width), lambda i: (i, 0)),
-            pl.BlockSpec((3, STEP, channels), lambda i: (0, i, 0)),
+            pl.BlockSpec((many, latent_width), lambda i: (i, 0)),
+            pl.BlockSpec((3, many, channels), lambda i: (0, i, 0)),
             whole((owners, atoms)),
         ),
         scratch_shapes=[
             pltpu.VMEM((owners * window, 5 * channels), bf16),
-            pltpu.VMEM((STEP, 5 * channels), f32),
+            pltpu.VMEM((many, 5 * channels), f32),
+            pltpu.VMEM((atoms, LANES), f32),
         ],
         compiler_params=pltpu.CompilerParams(dimension_semantics=("arbitrary",)),
         name="final",

time: 232 us -> 227 us (0.978)
  blocking collectives: 17.5 us -> 25.3 us
  waiting for transfers between devices: 125 us -> 119 us
  starting transfers between devices: 24.1 us -> 19.3 us
    all_to_all x0 -> x1, blocking collectives: none -> 14 us  [local(): lax.all_to_all(request, ('gy', 'gz'), split_axis=0, concat_axis=0, tiled=...]
    all_to_all x1, blocking collectives: 17.5 us -> 11.2 us  [local(): lax.all_to_all(sums, ('gy', 'gz'), split_axis=0, concat_axis=0, tiled=True)]
    all_to_all x1 -> x0, starting transfers between devices: 5.94 us -> none  [local(): lax.all_to_all(request, ('gy', 'gz'), split_axis=0, concat_axis=0, tiled=...]
    all_to_all x1 -> x0, waiting for transfers between devices: 5.63 us -> none  [local(): lax.all_to_all(request, ('gy', 'gz'), split_axis=0, concat_axis=0, tiled=...]
    ppermute x15 -> x18, starting transfers between devices: 10.4 us -> 12.9 us  [swap(): lax.ppermute(x, axis, [(i, i ^ bit) for i in range(lax.axis_size(axis))])]
    ppermute x15 -> x18, waiting for transfers between devices: 119 us -> 117 us  [swap(): lax.ppermute(x, axis, [(i, i ^ bit) for i in range(lax.axis_size(axis))])]
    pallas_call x1, Pallas kernels: 20.4 us -> 18.1 us  [local(): pl.pallas_call(functools.partial(final_kernel, owners, cap, window), grid...]
  transfers between devices with their start and end apart: 18 -> 20, of which waited for: 6 -> 7; matrix products, arithmetic and copies ran while one was open for 2% -> 3% of each run, Pallas kernels for 7% -> 7%
where the time goes in v3:
time: 227 us; the launch traced here: 226 us
  waiting for transfers between devices  119 us (52%)
  Pallas kernels  50.1 us (22%)
  blocking collectives  25.3 us (11%)
  starting transfers between devices  19.3 us (9%)
  local copies, waits for them, and re-layouts  7.97 us (4%)
  other arithmetic  2.95 us (1%)
    ppermute x18, waiting for transfers between devices, swap(): lax.ppermute(x, axis, [(i, i ^ bit) for i in range(lax.axis_size(axis))])  117 us
    pallas_call x1, Pallas kernels, local(): pl.pallas_call(functools.partial(final_kernel, owners, cap, window), grid...  18.1 us
    pallas_call x1, Pallas kernels, local(): pl.pallas_call(functools.partial(latent_kernel, basis), grid=(slots // ma...  16.2 us
    all_to_all x1, blocking collectives, local(): lax.all_to_all(request, ('gy', 'gz'), split_axis=0, concat_axis=0, tiled=...  14 us
    pallas_call x1, Pallas kernels, local(): pl.pallas_call(functools.partial(owner_kernel, cap), grid=(owners // grou...  13.7 us
    ppermute x18, starting transfers between devices, swap(): lax.ppermute(x, axis, [(i, i ^ bit) for i in range(lax.axis_size(axis))])  12.9 us
    all_to_all x1, blocking collectives, local(): lax.all_to_all(sums, ('gy', 'gz'), split_axis=0, concat_axis=0, tiled=True)  11.2 us
    all_to_all x1, starting transfers between devices, local(): lax.all_to_all(sent.reshape(owners, cap, 5 * channels), ('gy', 'gz'), spl...  4.84 us
  transfers between devices with their start and end apart: 20, of which 7 were waited for; matrix products, arithmetic and copies ran while one was open for 3% of the time, Pallas kernels for 7%

profile of v3, /device:TPU:0, one launch (start us, length us, event | category | flops | bytes accessed | tf_op | source)
XLA Modules:
  0.0 226.1 jit_solution(12726177270907476740)
XLA Ops:
  1.3 2.2 route.1
  3.4 14.0 %all_to_all.19.request_ref = f32[16,4,256]{2,1,0:T(4,128)S(1)} all-to-all(f32[16,4,256]{2,1,0:T(4,128)} %get-tuple-element.20), channel_id=1, replica_groups=mesh['gx'=2,'gy'=4,'gz'=4] {'gy','gz'}, dimensions={0} | all-to-all | bytes 131072 | tf_op jit(solution)/shard_map/all_to_all | solution.py:388
  17.5 0.1 slice.3
  17.6 0.1 reshape.92
  17.7 0.5 copy-done.4
  18.1 13.7 %owner.1 = bf16[3072,640]{1,0:T(8,128)(2,1)} custom-call(f32[16,4,256]{2,1,0:T(4,128)} %copy-done.4, bf16[9,1024,128]{2,1,0:T(8,128)(2,1)} %bitcast.38), custom_call_target="tpu_custom_call" | custom-call | flops 7247757312 | bytes 9437184 | tf_op jit(solution)/shard_map/owner/pallas_call | solution.py:399
  31.8 0.0 copy-start
  31.8 4.8 %all-to-all-start.1 = ((bf16[16,192,640]{2,1,0:T(8,128)(2,1)}), bf16[16,192,640]{2,1,0:T(8,128)(2,1)}, u32[]{:S(2)}, u32[]{:S(2)}) async-start(bf16[16,192,640]{2,1,0:T(8,128)(2,1)} %bitcast.25), calls=%async_computation.1 | async-start | bytes 7864320 | tf_op jit(solution)/shard_map/all_to_all | solution.py:422
  36.8 0.1 select_select_fusion
  36.8 1.7 collective-permute-start.8
  38.5 0.0 collective-permute-start.4
  38.5 3.3 %collective-permute-start.2 = (bf16[1024,128]{1,0:T(8,128)(2,1)S(1)}, bf16[1024,128]{1,0:T(8,128)(2,1)S(1)}, u32[]{:S(2)}, u32[]{:S(2)}) collective-permute-start(bf16[1024,128]{1,0:T(8,128)(2,1)S(1)} %copy-done), channel_id=1, source_target_pairs={{0,3},{1,2},{2,1},{3,0},{4,7},{5,6},{6,5},{7,4},{8,11},{9,10},{10,... | collective-permute-start | bytes 786440 | tf_op jit(solution)/shard_map/ppermute | solution.py:329
  41.8 0.0 collective-permute-start.1
  41.8 1.1 collective-permute-start
  42.9 0.6 gather_fusion
  43.5 0.1 add_bitcast_fusion
  43.6 67.3 %collective-permute-done.2.refs_3_ = bf16[1024,128]{1,0:T(8,128)(2,1)S(1)} collective-permute-done((bf16[1024,128]{1,0:T(8,128)(2,1)S(1)}, bf16[1024,128]{1,0:T(8,128)(2,1)S(1)}, u32[]{:S(2)}, u32[]{:S(2)}) %collective-permute-start.2) | collective-permute-done | bytes 262176 | tf_op jit(solution)/shard_map/ppermute | solution.py:329
  110.9 36.2 %collective-permute-done.1.refs_2_ = bf16[1024,128]{1,0:T(8,128)(2,1)S(1)} collective-permute-done((bf16[1024,128]{1,0:T(8,128)(2,1)S(1)}, bf16[1024,128]{1,0:T(8,128)(2,1)S(1)}, u32[]{:S(2)}, u32[]{:S(2)}) %collective-permute-start.1) | collective-permute-done | bytes 262176 | tf_op jit(solution)/shard_map/ppermute | solution.py:329
  147.1 0.0 collective-permute-done.refs_1_
  147.1 0.1 pad_maximum_fusion
  147.2 0.0 copy-start.10
  147.2 0.0 copy-start.5
  147.2 0.0 copy-start.6
  147.3 3.2 %gather_fusion.1 = bf16[1024,128]{1,0:T(8,128)(2,1)S(1)} fusion(bf16[4096,128]{1,0:T(8,128)(2,1)S(1)} %pad_maximum_fusion, s32[1024]{0:T(1024)S(1)} %broadcast_clamp_fusion), kind=kCustom, calls=%fused_computation.1 | custom fusion | bytes 528384 | tf_op jit(solution)/shard_map/gather | solution.py:434
  150.5 1.5 collective-permute-start.3
  152.0 1.5 collective-permute-start.11
  153.5 0.0 collective-permute-start.7
  153.5 0.0 collective-permute-done.8.refs_8_
  153.6 0.5 collective-permute-start.12
  154.1 0.4 copy.20
  154.4 1.3 reshape.96.index_ref
  155.7 0.7 pad_add_fusion.1.lists_ref
  156.4 1.9 collective-permute-done.3.refs_16_
  158.3 1.5 collective-permute-start.10
  159.8 0.0 collective-permute-done.4.refs_4_
  159.8 0.1 collective-permute-start.6
  159.9 0.0 collective-permute-done.12.refs_12_
  159.9 0.6 collective-permute-start.9
  160.5 0.0 collective-permute-done.11.refs_11_
  160.5 0.1 collective-permute-start.5
  160.7 0.0 collective-permute-done.7.refs_7_
  160.7 1.5 collective-permute-start.17
  162.2 5.3 %collective-permute-done.10.refs_10_ = bf16[1024,128]{1,0:T(8,128)(2,1)S(1)} collective-permute-done((bf16[1024,128]{1,0:T(8,128)(2,1)S(1)}, bf16[1024,128]{1,0:T(8,128)(2,1)S(1)}, u32[]{:S(2)}, u32[]{:S(2)}) %collective-permute-start.10) | collective-permute-done | bytes 262176 | tf_op jit(solution)/shard_map/ppermute | solution.py:329
  167.5 0.0 collective-permute-start.16
  167.5 0.0 collective-permute-done.6.refs_6_
  167.5 0.5 collective-permute-start.15
  168.0 5.1 %collective-permute-done.9.refs_9_ = bf16[1024,128]{1,0:T(8,128)(2,1)S(1)} collective-permute-done((bf16[1024,128]{1,0:T(8,128)(2,1)S(1)}, bf16[1024,128]{1,0:T(8,128)(2,1)S(1)}, u32[]{:S(2)}, u32[]{:S(2)}) %collective-permute-start.9) | collective-permute-done | bytes 262176 | tf_op jit(solution)/shard_map/ppermute | solution.py:329
  173.1 0.0 collective-permute-start.14
  173.1 0.0 collective-permute-done.5.refs_5_
  173.1 0.5 collective-permute-start.13
  173.6 2.9 %collective-permute-done.17.refs_18_ = bf16[1024,128]{1,0:T(8,128)(2,1)S(1)} collective-permute-done((bf16[1024,128]{1,0:T(8,128)(2,1)S(1)}, bf16[1024,128]{1,0:T(8,128)(2,1)S(1)}, u32[]{:S(2)}, u32[]{:S(2)}) %collective-permute-start.17) | collective-permute-done | bytes 262176 | tf_op jit(solution)/shard_map/ppermute | solution.py:329
  176.6 0.0 collective-permute-start.18
  176.6 0.7 pad_maximum_fusion.2.refs_21_
  177.2 0.7 pad_maximum_fusion.1.refs_20_
  178.0 0.0 collective-permute-done.15.refs_15_
  178.0 0.0 collective-permute-done.14.refs_14_
  178.0 0.0 collective-permute-done.13.refs_13_
  178.0 0.1 collective-permute-done.18.refs_19_
  178.1 0.9 copy-done.23
  179.1 16.2 %latent.1 = (bf16[2048,512]{1,0:T(8,128)(2,1)}, f32[2048,384]{1,0:T(8,128)}) custom-call(s32[6144]{0:T(1024)} %reshape.96.index_ref, s32[4097]{0:T(1024)} %pad_add_fusion.1.lists_ref, f32[8,2048]{1,0:T(8,128)} %get-tuple-element.19.rows_ref, bf16[1024,128]{1,0:T(8,128)(2,1)} %refs_0_, bf16[1024,128]{1,0:T(8,128)(2,1)} %copy-done.3, ...), custom_call_target="tpu_custom_call" | custom-call | flops 2952790016 | bytes 5242880 | tf_op jit(solution)/shard_map/latent/pallas_call | solution.py:472
  195.3 18.1 %final.1 = (bf16[2048,512]{1,0:T(8,128)(2,1)}, bf16[3,2048,128]{2,1,0:T(8,128)(2,1)}, f32[16,1024]{1,0:T(8,128)}) custom-call(s32[16,128]{1,0:T(8,128)} %get-tuple-element.18.starts_ref, f32[8,2048]{1,0:T(8,128)} %get-tuple-element.19.rows_ref, bf16[3072,640]{1,0:T(8,128)(2,1)} %bitcast.5.env_ref, f32[2048,384]{1,0:T(8,128)} %get-tuple-element.28.mixed_ref, ...), custom_call_target="tpu_custom_call" | custom-call | tf_op jit(solution)/shard_map/final/pallas_call | solution.py:511
  213.4 0.9 copy.21
  214.3 11.2 %all_to_all.20 = f32[16,1,1024]{2,1,0:T(1,128)S(1)} all-to-all(f32[16,1,1024]{2,1,0:T(1,128)S(1)} %copy.21), channel_id=1, replica_groups=mesh['gx'=2,'gy'=4,'gz'=4] {'gy','gz'}, dimensions={0} | all-to-all | bytes 131072 | tf_op jit(solution)/shard_map/all_to_all | solution.py:551
  225.5 0.6 reduce_sum.9
  (55 shorter events, 0.2 us)
Async XLA Ops:
  17.5 0.6 copy-start.4
  31.8 4.9 %copy-start.7 = (s32[2048,1]{0,1:T(1,128)S(1)}, s32[2048,1]{0,1:T(1,128)}, u32[]{:S(2)}) copy-start(s32[2048,1]{0,1:T(1,128)} %param.21) | copy-start | bytes 24580
  31.8 4.9 %copy-start.8 = (s32[2048]{0:T(1024)S(1)}, s32[2048]{0:T(1024)}, u32[]{:S(2)}) copy-start(s32[2048]{0:T(1024)} %param.20) | copy-start | bytes 24580
  31.8 4.9 %copy-start.9 = (s32[2048]{0:T(1024)S(1)}, s32[2048]{0:T(1024)}, u32[]{:S(2)}) copy-start(s32[2048]{0:T(1024)} %param.22) | copy-start | bytes 24580
  31.8 5.0 %copy-start = (bf16[1024,128]{1,0:T(8,128)(2,1)S(1)}, bf16[1024,128]{1,0:T(8,128)(2,1)}, u32[]{:S(2)}) copy-start(bf16[1024,128]{1,0:T(8,128)(2,1)} %refs_0_) | copy-start | bytes 786436
  31.8 163.5 %all-to-all-start.1 = ((bf16[16,192,640]{2,1,0:T(8,128)(2,1)}), bf16[16,192,640]{2,1,0:T(8,128)(2,1)}, u32[]{:S(2)}, u32[]{:S(2)}) async-start(bf16[16,192,640]{2,1,0:T(8,128)(2,1)} %bitcast.25), calls=%async_computation.1 | async-start | bytes 7864320 | tf_op jit(solution)/shard_map/all_to_all | solution.py:422
  36.8 116.7 %collective-permute-start.8 = (bf16[1024,128]{1,0:T(8,128)(2,1)S(1)}, bf16[1024,128]{1,0:T(8,128)(2,1)S(1)}, u32[]{:S(2)}, u32[]{:S(2)}) collective-permute-start(bf16[1024,128]{1,0:T(8,128)(2,1)S(1)} %copy-done), channel_id=1, source_target_pairs={{0,8},{4,12},{8,0},{12,4},{1,9},{5,13},{9,1},{13,5},{2,10},{6,14},... | collective-permute-start | bytes 786440 | tf_op jit(solution)/shard_map/ppermute | solution.py:329
  38.5 121.3 %collective-permute-start.4 = (bf16[1024,128]{1,0:T(8,128)(2,1)S(1)}, bf16[1024,128]{1,0:T(8,128)(2,1)S(1)}, u32[]{:S(2)}, u32[]{:S(2)}) collective-permute-start(bf16[1024,128]{1,0:T(8,128)(2,1)S(1)} %copy-done), channel_id=1, source_target_pairs={{0,4},{4,0},{8,12},{12,8},{1,5},{5,1},{9,13},{13,9},{2,6},{6,2},{1... | collective-permute-start | bytes 786440 | tf_op jit(solution)/shard_map/ppermute | solution.py:329
  38.5 72.4 %collective-permute-start.2 = (bf16[1024,128]{1,0:T(8,128)(2,1)S(1)}, bf16[1024,128]{1,0:T(8,128)(2,1)S(1)}, u32[]{:S(2)}, u32[]{:S(2)}) collective-permute-start(bf16[1024,128]{1,0:T(8,128)(2,1)S(1)} %copy-done), channel_id=1, source_target_pairs={{0,3},{1,2},{2,1},{3,0},{4,7},{5,6},{6,5},{7,4},{8,11},{9,10},{10,... | collective-permute-start | bytes 786440 | tf_op jit(solution)/shard_map/ppermute | solution.py:329
  41.8 105.3 %collective-permute-start.1 = (bf16[1024,128]{1,0:T(8,128)(2,1)S(1)}, bf16[1024,128]{1,0:T(8,128)(2,1)S(1)}, u32[]{:S(2)}, u32[]{:S(2)}) collective-permute-start(bf16[1024,128]{1,0:T(8,128)(2,1)S(1)} %copy-done), channel_id=1, source_target_pairs={{0,2},{1,3},{2,0},{3,1},{4,6},{5,7},{6,4},{7,5},{8,10},{9,11},{10,... | collective-permute-start | bytes 786440 | tf_op jit(solution)/shard_map/ppermute | solution.py:329
  41.8 105.3 %collective-permute-start = (bf16[1024,128]{1,0:T(8,128)(2,1)S(1)}, bf16[1024,128]{1,0:T(8,128)(2,1)S(1)}, u32[]{:S(2)}, u32[]{:S(2)}) collective-permute-start(bf16[1024,128]{1,0:T(8,128)(2,1)S(1)} %copy-done), channel_id=1, source_target_pairs={{0,1},{1,0},{2,3},{3,2},{4,5},{5,4},{6,7},{7,6},{8,9},{9,8},{10,11... | collective-permute-start | bytes 786440 | tf_op jit(solution)/shard_map/ppermute | solution.py:329
  110.9 42.6 %copy-start.1 = (bf16[1024,128]{1,0:T(8,128)(2,1)}, bf16[1024,128]{1,0:T(8,128)(2,1)S(1)}, u32[]{:S(2)}) copy-start(bf16[1024,128]{1,0:T(8,128)(2,1)S(1)} %collective-permute-done.2.refs_3_) | copy-start | bytes 786436
  147.1 12.7 %copy-start.2 = (bf16[1024,128]{1,0:T(8,128)(2,1)}, bf16[1024,128]{1,0:T(8,128)(2,1)S(1)}, u32[]{:S(2)}) copy-start(bf16[1024,128]{1,0:T(8,128)(2,1)S(1)} %collective-permute-done.1.refs_2_) | copy-start | bytes 786436
  147.1 13.4 %copy-start.3 = (bf16[1024,128]{1,0:T(8,128)(2,1)}, bf16[1024,128]{1,0:T(8,128)(2,1)S(1)}, u32[]{:S(2)}) copy-start(bf16[1024,128]{1,0:T(8,128)(2,1)S(1)} %collective-permute-done.refs_1_) | copy-start | bytes 786436
  147.2 29.4 %copy-start.10 = (bf16[8,512]{1,0:T(8,128)(2,1)S(1)}, bf16[8,512]{1,0:T(8,128)(2,1)}, u32[]{:S(2)}) copy-start(bf16[8,512]{1,0:T(8,128)(2,1)} %param.26) | copy-start | bytes 24580
  147.2 30.0 %copy-start.5 = (bf16[128,512]{1,0:T(8,128)(2,1)S(1)}, bf16[128,512]{1,0:T(8,128)(2,1)}, u32[]{:S(2)}) copy-start(bf16[128,512]{1,0:T(8,128)(2,1)} %param.25) | copy-start | bytes 393220
  147.2 30.0 %copy-start.6 = (bf16[128,512]{1,0:T(8,128)(2,1)S(1)}, bf16[128,512]{1,0:T(8,128)(2,1)}, u32[]{:S(2)}) copy-start(bf16[128,512]{1,0:T(8,128)(2,1)} %param.24) | copy-start | bytes 393220
  150.5 7.8 %collective-permute-start.3 = (bf16[1024,128]{1,0:T(8,128)(2,1)S(1)}, bf16[1024,128]{1,0:T(8,128)(2,1)S(1)}, u32[]{:S(2)}, u32[]{:S(2)}) collective-permute-start(bf16[1024,128]{1,0:T(8,128)(2,1)S(1)} %gather_fusion.1), channel_id=1, source_target_pairs={{0,16},{16,0},{1,17},{17,1},{2,18},{18,2},{3,19},{19,3},{4,20},{20... | collective-permute-start | bytes 786440 | tf_op jit(solution)/shard_map/ppermute | solution.py:437
  152.0 8.5 %collective-permute-start.11 = (bf16[1024,128]{1,0:T(8,128)(2,1)S(1)}, bf16[1024,128]{1,0:T(8,128)(2,1)}, u32[]{:S(2)}, u32[]{:S(2)}) collective-permute-start(bf16[1024,128]{1,0:T(8,128)(2,1)S(1)} %collective-permute-done.2.refs_3_), channel_id=1, source_target_pairs={{0,8},{4,12},{8,0},{12,4},{1,9},{5,13},{9,1},{13,5},{2,10},{6,14},... | collective-permute-start | bytes 786440 | tf_op jit(solution)/shard_map/ppermute | solution.py:329
  153.5 7.1 %collective-permute-start.7 = (bf16[1024,128]{1,0:T(8,128)(2,1)S(1)}, bf16[1024,128]{1,0:T(8,128)(2,1)}, u32[]{:S(2)}, u32[]{:S(2)}) collective-permute-start(bf16[1024,128]{1,0:T(8,128)(2,1)S(1)} %collective-permute-done.2.refs_3_), channel_id=1, source_target_pairs={{0,4},{4,0},{8,12},{12,8},{1,5},{5,1},{9,13},{13,9},{2,6},{6,2},{1... | collective-permute-start | bytes 786440 | tf_op jit(solution)/shard_map/ppermute | solution.py:329
  153.5 25.5 %copy-start.11 = (bf16[1024,128]{1,0:T(8,128)(2,1)}, bf16[1024,128]{1,0:T(8,128)(2,1)S(1)}, u32[]{:S(2)}) copy-start(bf16[1024,128]{1,0:T(8,128)(2,1)S(1)} %collective-permute-done.8.refs_8_) | copy-start | bytes 786436
  153.6 6.4 %collective-permute-start.12 = (bf16[1024,128]{1,0:T(8,128)(2,1)S(1)}, bf16[1024,128]{1,0:T(8,128)(2,1)}, u32[]{:S(2)}, u32[]{:S(2)}) collective-permute-start(bf16[1024,128]{1,0:T(8,128)(2,1)S(1)} %collective-permute-done.8.refs_8_), channel_id=1, source_target_pairs={{0,4},{4,0},{8,12},{12,8},{1,5},{5,1},{9,13},{13,9},{2,6},{6,2},{1... | collective-permute-start | bytes 786440 | tf_op jit(solution)/shard_map/ppermute | solution.py:329
  158.3 20.7 %copy-start.13 = (bf16[1024,128]{1,0:T(8,128)(2,1)}, bf16[1024,128]{1,0:T(8,128)(2,1)S(1)}, u32[]{:S(2)}) copy-start(bf16[1024,128]{1,0:T(8,128)(2,1)S(1)} %collective-permute-done.3.refs_16_) | copy-start | bytes 786436
  158.3 9.2 %collective-permute-start.10 = (bf16[1024,128]{1,0:T(8,128)(2,1)S(1)}, bf16[1024,128]{1,0:T(8,128)(2,1)S(1)}, u32[]{:S(2)}, u32[]{:S(2)}) collective-permute-start(bf16[1024,128]{1,0:T(8,128)(2,1)S(1)} %collective-permute-done.1.refs_2_), channel_id=1, source_target_pairs={{0,8},{4,12},{8,0},{12,4},{1,9},{5,13},{9,1},{13,5},{2,10},{6,14},... | collective-permute-start | bytes 786440 | tf_op jit(solution)/shard_map/ppermute | solution.py:329
  159.8 19.2 %copy-start.12 = (bf16[1024,128]{1,0:T(8,128)(2,1)}, bf16[1024,128]{1,0:T(8,128)(2,1)S(1)}, u32[]{:S(2)}) copy-start(bf16[1024,128]{1,0:T(8,128)(2,1)S(1)} %collective-permute-done.4.refs_4_) | copy-start | bytes 786436
  159.8 7.7 %collective-permute-start.6 = (bf16[1024,128]{1,0:T(8,128)(2,1)S(1)}, bf16[1024,128]{1,0:T(8,128)(2,1)S(1)}, u32[]{:S(2)}, u32[]{:S(2)}) collective-permute-start(bf16[1024,128]{1,0:T(8,128)(2,1)S(1)} %collective-permute-done.1.refs_2_), channel_id=1, source_target_pairs={{0,4},{4,0},{8,12},{12,8},{1,5},{5,1},{9,13},{13,9},{2,6},{6,2},{1... | collective-permute-start | bytes 786440 | tf_op jit(solution)/shard_map/ppermute | solution.py:329
  159.9 13.2 %collective-permute-start.9 = (bf16[1024,128]{1,0:T(8,128)(2,1)S(1)}, bf16[1024,128]{1,0:T(8,128)(2,1)S(1)}, u32[]{:S(2)}, u32[]{:S(2)}) collective-permute-start(bf16[1024,128]{1,0:T(8,128)(2,1)S(1)} %collective-permute-done.refs_1_), channel_id=1, source_target_pairs={{0,8},{4,12},{8,0},{12,4},{1,9},{5,13},{9,1},{13,5},{2,10},{6,14},... | collective-permute-start | bytes 786440 | tf_op jit(solution)/shard_map/ppermute | solution.py:329
  160.5 12.6 %collective-permute-start.5 = (bf16[1024,128]{1,0:T(8,128)(2,1)S(1)}, bf16[1024,128]{1,0:T(8,128)(2,1)S(1)}, u32[]{:S(2)}, u32[]{:S(2)}) collective-permute-start(bf16[1024,128]{1,0:T(8,128)(2,1)S(1)} %collective-permute-done.refs_1_), channel_id=1, source_target_pairs={{0,4},{4,0},{8,12},{12,8},{1,5},{5,1},{9,13},{13,9},{2,6},{6,2},{1... | collective-permute-start | bytes 786440 | tf_op jit(solution)/shard_map/ppermute | solution.py:329
  160.7 15.9 %collective-permute-start.17 = (bf16[1024,128]{1,0:T(8,128)(2,1)S(1)}, bf16[1024,128]{1,0:T(8,128)(2,1)S(1)}, u32[]{:S(2)}, u32[]{:S(2)}) collective-permute-start(bf16[1024,128]{1,0:T(8,128)(2,1)S(1)} %collective-permute-done.3.refs_16_), channel_id=1, source_target_pairs={{0,8},{4,12},{8,0},{12,4},{1,9},{5,13},{9,1},{13,5},{2,10},{6,14},... | collective-permute-start | bytes 786440 | tf_op jit(solution)/shard_map/ppermute | solution.py:329
  167.5 11.5 %copy-start.14 = (bf16[1024,128]{1,0:T(8,128)(2,1)}, bf16[1024,128]{1,0:T(8,128)(2,1)S(1)}, u32[]{:S(2)}) copy-start(bf16[1024,128]{1,0:T(8,128)(2,1)S(1)} %collective-permute-done.10.refs_10_) | copy-start | bytes 786436
  167.5 10.5 %collective-permute-start.16 = (bf16[1024,128]{1,0:T(8,128)(2,1)S(1)}, bf16[1024,128]{1,0:T(8,128)(2,1)S(1)}, u32[]{:S(2)}, u32[]{:S(2)}) collective-permute-start(bf16[1024,128]{1,0:T(8,128)(2,1)S(1)} %collective-permute-done.3.refs_16_), channel_id=1, source_target_pairs={{0,4},{4,0},{8,12},{12,8},{1,5},{5,1},{9,13},{13,9},{2,6},{6,2},{1... | collective-permute-start | bytes 786440 | tf_op jit(solution)/shard_map/ppermute | solution.py:329
  167.5 11.5 %copy-start.15 = (bf16[1024,128]{1,0:T(8,128)(2,1)}, bf16[1024,128]{1,0:T(8,128)(2,1)S(1)}, u32[]{:S(2)}) copy-start(bf16[1024,128]{1,0:T(8,128)(2,1)S(1)} %collective-permute-done.6.refs_6_) | copy-start | bytes 786436
  167.5 10.4 %collective-permute-start.15 = (bf16[1024,128]{1,0:T(8,128)(2,1)}, bf16[1024,128]{1,0:T(8,128)(2,1)S(1)}, u32[]{:S(2)}, u32[]{:S(2)}) collective-permute-start(bf16[1024,128]{1,0:T(8,128)(2,1)} %collective-permute-done.11.refs_11_), channel_id=1, source_target_pairs={{0,4},{4,0},{8,12},{12,8},{1,5},{5,1},{9,13},{13,9},{2,6},{6,2},{1... | collective-permute-start | bytes 786440 | tf_op jit(solution)/shard_map/ppermute | solution.py:329
  173.1 5.9 %copy-start.16 = (bf16[1024,128]{1,0:T(8,128)(2,1)}, bf16[1024,128]{1,0:T(8,128)(2,1)S(1)}, u32[]{:S(2)}) copy-start(bf16[1024,128]{1,0:T(8,128)(2,1)S(1)} %collective-permute-done.9.refs_9_) | copy-start | bytes 786436
  173.1 4.9 %collective-permute-start.14 = (bf16[1024,128]{1,0:T(8,128)(2,1)S(1)}, bf16[1024,128]{1,0:T(8,128)(2,1)S(1)}, u32[]{:S(2)}, u32[]{:S(2)}) collective-permute-start(bf16[1024,128]{1,0:T(8,128)(2,1)S(1)} %collective-permute-done.10.refs_10_), channel_id=1, source_target_pairs={{0,4},{4,0},{8,12},{12,8},{1,5},{5,1},{9,13},{13,9},{2,6},{6,2},{1... | collective-permute-start | bytes 786440 | tf_op jit(solution)/shard_map/ppermute | solution.py:329
  173.1 5.9 %copy-start.17 = (bf16[1024,128]{1,0:T(8,128)(2,1)}, bf16[1024,128]{1,0:T(8,128)(2,1)S(1)}, u32[]{:S(2)}) copy-start(bf16[1024,128]{1,0:T(8,128)(2,1)S(1)} %collective-permute-done.5.refs_5_) | copy-start | bytes 786436
  173.1 4.8 %collective-permute-start.13 = (bf16[1024,128]{1,0:T(8,128)(2,1)S(1)}, bf16[1024,128]{1,0:T(8,128)(2,1)S(1)}, u32[]{:S(2)}, u32[]{:S(2)}) collective-permute-start(bf16[1024,128]{1,0:T(8,128)(2,1)S(1)} %collective-permute-done.9.refs_9_), channel_id=1, source_target_pairs={{0,4},{4,0},{8,12},{12,8},{1,5},{5,1},{9,13},{13,9},{2,6},{6,2},{1... | collective-permute-start | bytes 786440 | tf_op jit(solution)/shard_map/ppermute | solution.py:329
  176.6 2.5 %copy-start.18 = (bf16[1024,128]{1,0:T(8,128)(2,1)}, bf16[1024,128]{1,0:T(8,128)(2,1)S(1)}, u32[]{:S(2)}) copy-start(bf16[1024,128]{1,0:T(8,128)(2,1)S(1)} %collective-permute-done.17.refs_18_) | copy-start | bytes 786436
  176.6 1.5 collective-permute-start.18
  178.0 1.1 copy-start.20
  178.0 1.1 copy-start.21
  178.0 1.1 copy-start.22
  178.0 1.1 copy-start.19
  178.1 0.9 copy-start.23
